TPU v7x, 1024 devices: a whole 8x8x8 slice. The times are simulated.
1024 devices in a mesh: fsdp: 16 (over y, z_hi), rep: 64 (over z_lo, x, core).
Axes of the slice: x: 8, y: 8, z: 8 (z_hi: 2, z_lo: 4; z = z_hi * 4 + z_lo), core: 2. Of those that a mesh axis runs over, the one named last changes fastest.
Arguments:
- hidden_in: bfloat16 [262144, 2048], P(('fsdp', 'rep'))
- out_grad: bfloat16 [262144, 2048], P(('fsdp', 'rep')), may hold values from -6 to 6
- attn_saved: bfloat16 [262144, 256], P(('fsdp', 'rep')), may hold values from -6 to 6
- row_lse: float32 [262144, 2], P(('fsdp', 'rep')), may hold values from 2.5 to 6
- w_qkv: bfloat16 [2048, 512], P('fsdp'), may hold values from -0.125 to 0.125
- w_out_t: bfloat16 [2048, 256], P('fsdp'), may hold values from -0.125 to 0.125
- doc_lengths: int32 [1024, 4], P(('fsdp', 'rep')), may hold values from 1 to 128, 256 in all within a row
- seq_start: int32 [1024], P(('fsdp', 'rep')), may hold values from 0 to 2047
Outputs:
- input_grad: bfloat16 [262144, 2048], P(('fsdp', 'rep'))
- grad_update: float32 [2048, 768], P('fsdp')
- grad_norm: float32 [], replicated
Inputs may be any that keep to these rules, and one draw needn't show every extreme that they name: `doc_lengths`: each row sums to 256; the longest document of each device has exactly 128 tokens.
All inputs are finite; a program needn't handle non-finite values.
Results may differ from a plain program's by a relative error of at most 0.014.
Values may be sent and summed in bfloat16 or wider, within the bound.
A program may use at most 64 MiB of HBM per device.

v0:
```python
import jax
import jax.numpy as jnp
from jax import lax
from jax.sharding import Mesh
from jax.sharding import PartitionSpec as P

D = 2048
HEAD = 128
FSDP = ("fsdp_0", "fsdp_1")
REP = ("rep_0", "rep_1", "rep_2")
FSDP_REP = ("fsdp_0", "fsdp_1", "rep_0", "rep_1", "rep_2")


def sent_together(arrays, axis, dim, along):
    both = jnp.concatenate(arrays, axis=along)
    whole, at, outs = (lax.all_gather(both, axis, axis=dim, tiled=True), 0, [])
    for a in arrays:
        outs.append(lax.slice_in_dim(whole, at, at + a.shape[along], axis=along))
        at += a.shape[along]
    return tuple(outs)


def in_blocks(array, dim, devices):
    before, after = (array.shape[:dim], array.shape[dim + 1 :])
    return jnp.moveaxis(array.reshape(*before, devices, -1, *after), dim, 0)


def summed_rows_2(array, chips, core, dim):
    sizes = (lax.axis_size(chips), lax.axis_size(core))
    tiles = in_blocks(array, dim, sizes[0] * sizes[1])
    inside = tiles.shape[1:]
    tiles = tiles.reshape(*sizes, *inside).swapaxes(0, 1).reshape(-1, *inside)
    tiles = lax.psum_scatter(tiles, core, scatter_dimension=0, tiled=True)
    return lax.psum_scatter(tiles, chips, scatter_dimension=0, tiled=True)[0]


def copy_for_each(array, axis):
    copies = jnp.broadcast_to(array, (lax.axis_size(axis), *array.shape))
    return lax.all_to_all(copies, axis, split_axis=0, concat_axis=0, tiled=True)


def in_order(tiles, dim):
    lengths = list(tiles.shape[1:])
    lengths[dim] *= tiles.shape[0]
    return jnp.moveaxis(tiles, 0, dim).reshape(lengths)


def gather_directly(array, axis, dim):
    tiles = copy_for_each(array, axis)
    return in_order(tiles, dim)


def taken_together(array, axis):
    return copy_for_each(array, axis).sum(axis=0)


def rotary(values_in, positions, turn, head_size):
    rows = values_in.shape[0]
    heads_count = values_in.shape[1] // head_size
    half_size = head_size // 2
    inverse = 1000000.0 ** (-(jnp.arange(half_size, dtype=jnp.float32) * 2.0) / head_size)
    angles = positions.astype(jnp.float32)[:, None] * inverse[None, :]
    cosine = jnp.cos(angles)[:, None, :]
    sines = jnp.sin(angles)[:, None, :]
    shaped = values_in.reshape(rows, heads_count, head_size)
    first_half = shaped[:, :, :half_size]
    second_half = shaped[:, :, half_size:]
    result = jnp.concatenate(
        [
            first_half * cosine - turn * second_half * sines,
            second_half * cosine + turn * first_half * sines,
        ],
        axis=2,
    )
    return result.reshape(rows, heads_count * head_size)


def contract_rows(left, right):
    return lax.dot_general(
        left, right, (((0,), (0,)), ((), ())), preferred_element_type=jnp.float32
    )


def contract_cols(left, right):
    return lax.dot_general(
        left, right, (((1,), (1,)), ((), ())), preferred_element_type=jnp.float32
    )


def body(hidden_in, out_grad, attn_saved, row_lse, w_qkv, w_out_t, doc_lengths, seq_start):
    seq_rows = hidden_in.shape[0]
    head_size = HEAD
    query_width = attn_saved.shape[1]
    heads_count = row_lse.shape[1]
    scale = 1.0 / head_size**0.5
    whole_qkv, whole_out = sent_together((w_qkv, w_out_t), FSDP, 0, 1)
    proj = jnp.dot(hidden_in, whole_qkv, preferred_element_type=jnp.float32)
    attn_full = jnp.dot(out_grad, whole_out, preferred_element_type=jnp.float32)
    attn_grad = attn_full.astype(jnp.bfloat16)
    positions = seq_start[0] + jnp.arange(seq_rows, dtype=jnp.int32)
    queries = rotary(proj[:, :query_width], positions, 1.0, head_size).astype(jnp.bfloat16)
    keys = rotary(proj[:, query_width : query_width + head_size], positions, 1.0, head_size).astype(
        jnp.bfloat16
    )
    values_all = proj[:, query_width + head_size :].astype(jnp.bfloat16)
    ends = jnp.cumsum(doc_lengths[0])
    local_rows = jnp.arange(seq_rows, dtype=jnp.int32)
    documents = jnp.sum((local_rows[:, None] >= ends[None, :]).astype(jnp.int32), axis=1)
    block_rows = min(seq_rows, 512)
    block_count = seq_rows // block_rows

    def attend_block(carry, inputs):
        key_grad, value_grad = carry
        query_rows, grad_rows, saved_rows, lse_rows, index_rows, doc_rows = inputs
        allowed = (doc_rows[:, None] == documents[None, :]) & (
            local_rows[None, :] <= index_rows[:, None]
        )
        query_parts = []
        for head_index in range(heads_count):
            lower = head_index * head_size
            query_head = query_rows[:, lower : lower + head_size]
            scores = contract_cols(query_head, keys) * scale
            probs = jnp.where(
                allowed, jnp.exp(scores - lse_rows[:, head_index : head_index + 1]), 0.0
            )
            grad_head = grad_rows[:, lower : lower + head_size]
            dprobs = contract_cols(grad_head, values_all)
            delta = jnp.sum(
                grad_head.astype(jnp.float32)
                * saved_rows[:, lower : lower + head_size].astype(jnp.float32),
                axis=1,
                keepdims=True,
            )
            dscores = (probs * (dprobs - delta) * scale).astype(jnp.bfloat16)
            probs_low = probs.astype(jnp.bfloat16)
            value_grad = value_grad + contract_rows(probs_low, grad_head)
            query_parts.append(jnp.dot(dscores, keys, preferred_element_type=jnp.float32))
            key_grad = key_grad + contract_rows(dscores, query_head)
        return ((key_grad, value_grad), jnp.concatenate(query_parts, axis=1))

    block_inputs = (
        queries.reshape(block_count, block_rows, query_width),
        attn_grad.reshape(block_count, block_rows, query_width),
        attn_saved.reshape(block_count, block_rows, query_width),
        row_lse.reshape(block_count, block_rows, heads_count),
        local_rows.reshape(block_count, block_rows),
        documents.reshape(block_count, block_rows),
    )
    zero_grad = jnp.zeros((seq_rows, head_size), jnp.float32)
    (key_grad, value_grad), query_blocks = lax.scan(
        attend_block, (zero_grad, zero_grad), block_inputs
    )
    query_grad = rotary(
        query_blocks.reshape(seq_rows, query_width), positions, -1.0, head_size
    ).astype(jnp.bfloat16)
    key_grad = rotary(key_grad, positions, -1.0, head_size).astype(jnp.bfloat16)
    d_qkv = jnp.concatenate([query_grad, key_grad, value_grad.astype(jnp.bfloat16)], axis=1)
    input_full = contract_cols(d_qkv, whole_qkv)
    input_grad = input_full.astype(jnp.bfloat16)
    member_count = lax.axis_size(FSDP) * lax.axis_size(REP)
    width_total = hidden_in.shape[1] * (d_qkv.shape[1] + attn_saved.shape[1])
    piece_width = width_total // member_count
    full_term = jnp.concatenate(
        [contract_rows(hidden_in, d_qkv), contract_rows(out_grad, attn_saved)], axis=1
    )
    rounded_term = lax.optimization_barrier(full_term.astype(jnp.bfloat16)).astype(jnp.float32)
    flat_term = rounded_term.reshape(member_count, piece_width)
    own_piece = summed_rows_2(flat_term, ("fsdp_0", "fsdp_1", "rep_0", "rep_1"), "rep_2", 0)
    gathered = gather_directly(own_piece, REP, 0)
    grads = gathered.reshape(w_qkv.shape[0], d_qkv.shape[1] + attn_saved.shape[1])
    norm_sq = taken_together(jnp.sum(grads * grads), FSDP)
    grad_update = grads * lax.rsqrt(norm_sq / (D * grads.shape[1]) + 1e-06)
    return (input_grad, grad_update, jnp.sqrt(norm_sq))


def solution(mesh):
    split = Mesh(
        mesh.devices.reshape(8, 2, 4, 8, 2), ("fsdp_0", "fsdp_1", "rep_0", "rep_1", "rep_2")
    )
    in_specs = (
        P(FSDP_REP, None),
        P(FSDP_REP, None),
        P(FSDP_REP, None),
        P(FSDP_REP, None),
        P(FSDP, None),
        P(FSDP, None),
        P(FSDP_REP, None),
        P(FSDP_REP),
    )
    out_specs = (P(FSDP_REP, None), P(FSDP, None), P())
    return jax.shard_map(body, mesh=split, in_specs=in_specs, out_specs=out_specs, check_vma=False)
```

profile of v0, /device:TPU:1, one launch (start us, length us, event | category | flops | bytes accessed | tf_op | source)
XLA Modules:
  0.0 525.9 jit_solution(14947228595045912211)
XLA Ops:
  7.2 1.7 pad_maximum_fusion.3
  9.7 0.9 fusion.56
  10.8 0.8 reduce-window.8
  11.7 0.8 fusion.57
  12.8 1.7 convolution_convert_fusion.2
  14.5 132.6 %all-gather.2.cloned.1.call-done = bf16[2048,768]{1,0:T(8,128)(2,1)} async-done(((bf16[128,768]{1,0:T(8,128)(2,1)}), bf16[2048,768]{1,0:T(8,128)(2,1)}) %all-gather.2.cloned.1.call-update) | async-done | bytes 3145744 | tf_op jit(solution)/shard_map/all_gather | solution.py:16
  147.1 2.3 fusion.4
  150.2 1.7 fusion.20
  154.8 1.9 pad_maximum_fusion
  156.8 5.4 %copy.27 = f32[2048,768]{1,0:T(8,128)} copy(bf16[2048,768]{0,1:T(8,128)(2,1)} %pad_maximum_fusion) | data formatting | bytes 9437184 | tf_op jit(solution)/shard_map/reshape | solution.py:32
  162.2 8.2 %reshape.197 = f32[512,2,1,1536]{3,1,0,2:T(2,128)} reshape(f32[2048,768]{1,0:T(8,128)} %copy.27) | data formatting | bytes 12582912 | tf_op jit(solution)/shard_map/reshape | solution.py:32
  170.4 6.7 %copy.28 = f32[2,512,1,1536]{3,1,0,2:T(8,128)} copy(f32[2,512,1,1536]{3,0,1,2:T(2,128)} %bitcast.41) | data formatting | bytes 12582912 | tf_op jit(solution)/shard_map/reshape | solution.py:32
  177.1 24.0 %reduce-scatter.3.cloned.1.call-done = f32[512,1,1536]{2,0,1:T(8,128)} async-done(((f32[1024,1,1536]{2,0,1:T(8,128)}), f32[512,1,1536]{2,0,1:T(8,128)}) %reduce-scatter.3.cloned.1.call-update) | async-done | bytes 3145744 | tf_op jit(solution)/shard_map/reduce_scatter | solution.py:33
  201.1 1.3 dynamic-slice.5
  202.4 262.8 %all-reduce.3.cloned.1.call-done = f32[512,1,1536]{2,0,1:T(8,128)} async-done(((f32[512,1,1536]{2,0,1:T(8,128)}), f32[512,1,1536]{2,0,1:T(8,128)}) %all-reduce.3.cloned.1.call-update) | async-done | bytes 3145744
  465.1 1.5 dynamic-slice_reduce_fusion
  466.8 26.8 %all_to_all.11 = f32[64,1,1536]{2,1,0:T(1,128)S(1)} all-to-all(f32[64,1,1536]{2,1,0:T(1,128)S(1)} %broadcast_in_dim.19), channel_id=1, replica_groups=mesh['fsdp_0'=8,'fsdp_1'=2,'rep_0'=4,'rep_1'=8,'rep_2'=2] {'rep_0','rep_..., dimensions={0} | all-to-all | bytes 786432 | tf_op jit(solution)/shard_map/all_to_all | solution.py:39
  493.6 1.4 multiply_reduce_fusion.1
  495.1 1.2 broadcast_in_dim.20
  496.3 6.8 %all-to-all-start.1 = ((f32[16,1,1]{2,1,0:T(1,128)}), f32[16,1,1]{2,1,0:T(1,128)S(1)}, u32[]{:S(2)}, u32[]{:S(2)}) async-start(f32[16,1,1]{2,1,0:T(1,128)} %broadcast_in_dim.20), calls=%async_computation.2 | async-start | bytes 16384 | tf_op jit(solution)/shard_map/all_to_all | solution.py:39
  503.1 3.3 convolution_convert_fusion.1
  506.5 7.9 %all-to-all-done.1 = f32[16,1,1]{2,1,0:T(1,128)S(1)} async-done(((f32[16,1,1]{2,1,0:T(1,128)}), f32[16,1,1]{2,1,0:T(1,128)S(1)}, u32[]{:S(2)}, u32[]{:S(2)}) %all-to-all-start.1) | async-done | bytes 96 | tf_op jit(solution)/shard_map/all_to_all | solution.py:39
  516.3 1.1 multiply_reduce_fusion
  517.4 0.8 mul.241
  (40 shorter events, 5.1 us)
Async XLA Ops:
  7.2 140.0 %copy-start = (bf16[256,2048]{1,0:T(8,128)(2,1)S(1)}, bf16[256,2048]{1,0:T(8,128)(2,1)}, u32[]{:S(2)}) copy-start(bf16[256,2048]{1,0:T(8,128)(2,1)} %param.8) | copy-start | bytes 3145732
  7.2 139.9 %all-gather.2.cloned.1.call-start = ((), (), s32[]{:S(2)}) async-start(), calls=%async_computation.3 | async-start | bytes 3342336 | tf_op jit(solution)/shard_map/all_gather | solution.py:16
  9.0 192.1 %reduce-scatter.3.cloned.1.call-start = ((), (), s32[]{:S(2)}) async-start(), calls=%async_computation.4 | async-start | bytes 9437184 | tf_op jit(solution)/shard_map/reduce_scatter | solution.py:33
  14.5 135.7 %copy-start.1 = (bf16[256,2048]{1,0:T(8,128)(2,1)S(1)}, bf16[256,2048]{1,0:T(8,128)(2,1)}, u32[]{:S(2)}) copy-start(bf16[256,2048]{1,0:T(8,128)(2,1)} %param.9) | copy-start | bytes 3145732
  177.0 288.1 %all-reduce.3.cloned.1.call-start = ((), (), s32[]{:S(2)}) async-start(), calls=%async_computation.5 | async-start | bytes 6291456
  496.3 18.1 %all-to-all-start.1 = ((f32[16,1,1]{2,1,0:T(1,128)}), f32[16,1,1]{2,1,0:T(1,128)S(1)}, u32[]{:S(2)}, u32[]{:S(2)}) async-start(f32[16,1,1]{2,1,0:T(1,128)} %broadcast_in_dim.20), calls=%async_computation.2 | async-start | bytes 16384 | tf_op jit(solution)/shard_map/all_to_all | solution.py:39
Sparse Core Ops, SparseCore 0:
  12.9 134.1 all-gather.1
  177.2 23.8 reduce-scatter.2
  205.8 259.3 all-reduce.2
where the time goes:
time: 527 us; the launch traced here: 526 us
  waiting for transfers between devices  427 us (81%)
  local copies, waits for them, and re-layouts  27.2 us (5%)
  blocking collectives  26.8 us (5%)
  between operations  17.2 us (3%)
  matrix products  11.7 us (2%)
  other arithmetic  8.77 us (2%)
  starting transfers between devices  6.96 us (1%)
    unnamed x4, waiting for transfers between devices  263 us
    all_gather x1, waiting for transfers between devices, sent_together(): whole, at, outs = (lax.all_gather(both, axis, axis=dim, tiled=True), 0, [])  133 us
    all_to_all x1, blocking collectives, copy_for_each(): return lax.all_to_all(copies, axis, split_axis=0, concat_axis=0, tiled=True)  26.8 us
    reduce_scatter x1, waiting for transfers between devices, summed_rows_2(): tiles = lax.psum_scatter(tiles, core, scatter_dimension=0, tiled=True)  24 us
    reshape x3, local copies, waits for them, and re-layouts, summed_rows_2(): tiles = tiles.reshape(*sizes, *inside).swapaxes(0, 1).reshape(-1, *inside)  20.2 us
  transfers between devices with their start and end apart: 4, of which 4 were waited for; matrix products, arithmetic and copies ran while one was open for 2% of the time, Pallas kernels for 0%

commit v1 on v0

v1 whole, which is shorter than its diff:
```python
import jax
import jax.numpy as jnp
import numpy as np
from jax import lax
from jax.experimental import pallas as pl
from jax.experimental.pallas import tpu as pltpu
from jax.sharding import Mesh
from jax.sharding import PartitionSpec as P

D = 2048
HEAD = 128
ROWS = 256
AXES = ("fsdp_0", "fsdp_1", "rep_0", "rep_1", "rep_2")
FSDP = AXES[:2]
FSDP_REP = AXES
F32 = jnp.float32
BF16 = jnp.bfloat16
SEMS = 360


def mod(value, size):
    return lax.rem(value + size, size)


def dot(left, right, contract=((1,), (0,))):
    return lax.dot_general(left, right, (contract, ((), ())), preferred_element_type=F32)


class Links:
    def __init__(self, sems):
        self.sems, self.used, self.started = sems, 0, []

    def send(self, src, dst, device):
        at = self.used
        self.used += 2
        copy = pltpu.make_async_remote_copy(
            src_ref=src,
            dst_ref=dst,
            send_sem=self.sems.at[at],
            recv_sem=self.sems.at[at + 1],
            device_id=device,
            device_id_type=pl.DeviceIdType.MESH,
        )
        copy.start()
        self.started.append(copy)
        return copy

    def finish(self):
        for copy in self.started:
            copy.wait_send()


def arrived(copies):
    for copy in copies:
        copy.wait_recv()


def kernel(
    start_ref,
    doc_ref,
    inv_ref,
    lse_ref,
    hid_hbm,
    og_hbm,
    as_hbm,
    wq_hbm,
    wo_hbm,
    ig_hbm,
    grads_ref,
    norm_ref,
    hid,
    og,
    saved,
    wbuf,
    hid_t,
    og_t,
    proj,
    cos_ref,
    sin_ref,
    dqkv,
    igv,
    gs_y,
    gs_x,
    gs_z,
    gr_y,
    gr_x,
    gr_z,
    s_y,
    s_x,
    s_z,
    r_y,
    r_x,
    r_z,
    s2_y,
    s2_x,
    s2_z,
    r2_y,
    r2_x,
    r2_z,
    r3_y,
    s3_x,
    r3_x,
    r3_z,
    fa,
    fx,
    nz,
    ny,
    sems,
    local,
):
    y = lax.axis_index(AXES[0])
    zh = lax.axis_index(AXES[1])
    zl = lax.axis_index(AXES[2])
    x = lax.axis_index(AXES[3])
    c = lax.axis_index(AXES[4])
    z = zh * 4 + zl
    mate = (y, zh, zl, x, 1 - c)
    mirror = (y, 1 - zh, 3 - zl, x, c)

    def at_y(d):
        return (mod(y + d, 8), zh, zl, x, c)

    def at_x(d, dc=0):
        return (y, zh, zl, mod(x + d, 8), mod(c + dc, 2))

    def at_z(d):
        there = mod(z + d, 8)
        return (y, there // 4, lax.rem(there, 4), x, c)

    def at_zl(d, dc):
        return (y, zh, mod(zl + d, 4), x, mod(c + dc, 2))

    peers = [mate]
    peers += [at_y(d) for d in range(1, 8)]
    peers += [at_x(d, dc) for d in range(1, 8) for dc in range(2)]
    peers += [at_z(d) for d in range(1, 8)]
    peers += [at_zl(d, 1) for d in range(1, 4)]
    barrier = pltpu.get_barrier_semaphore()
    extra = len(peers)
    for peer in peers:
        pl.semaphore_signal(barrier, inc=1, device_id=peer, device_id_type=pl.DeviceIdType.MESH)

    def rows_of(block, first, count):
        return pl.ds(pl.multiple_of(block * 128 + first, 32), count)

    own = y * 2 + zh
    own_rows = rows_of(own, 0, 128)
    load_wq = pltpu.make_async_copy(wq_hbm, wbuf.at[own_rows, pl.ds(0, 512)], local.at[0])
    load_wo = pltpu.make_async_copy(wo_hbm, wbuf.at[own_rows, pl.ds(512, 256)], local.at[1])
    load_og = pltpu.make_async_copy(og_hbm, og, local.at[2])
    load_as = pltpu.make_async_copy(as_hbm, saved, local.at[3])
    load_hid = pltpu.make_async_copy(hid_hbm, hid, local.at[4])
    for copy in (load_wq, load_wo, load_og, load_as, load_hid):
        copy.start()
    load_wq.wait()
    load_wo.wait()
    pl.semaphore_wait(barrier, extra)

    links = Links(sems)

    def weight(block, first, count, device):
        ref = wbuf.at[rows_of(block, first, count), :]
        return links.send(ref, ref, device)

    half = c * 64
    other_half = 1 - zh
    to_mirror = weight(own, half, 64, mirror)
    up, down = at_y(1), at_y(-1)
    shared = []

    class Ring:
        def __init__(self, zside):
            self.zside = zside
            self.sent = [self.pass_on(0)]

        def block(self, d):
            return mod(y + d, 8) * 2 + self.zside

        def pass_on(self, s):
            if s < 3:
                return (
                    weight(self.block(-s), half, 64, up),
                    weight(self.block(s), half, 64, down),
                )
            return (
                weight(self.block(-3), half, 32, up),
                weight(self.block(3), half + 32, 32, down),
            )

        def step(self, s):
            arrived(self.sent[-1])
            if s < 4:
                self.sent.append(self.pass_on(s))
                shared.append(weight(self.block(-s), half, 64, mate))
                shared.append(weight(self.block(s), half, 64, mate))
            else:
                shared.append(weight(self.block(4), half, 64, mate))

    ring_a = Ring(zh)

    positions = (start_ref[0] + lax.broadcasted_iota(jnp.int32, (ROWS, HEAD), 0)).astype(F32)
    angles = positions * inv_ref[...]
    sign = jnp.where(lax.broadcasted_iota(jnp.int32, (ROWS, HEAD), 1) < HEAD // 2, -1.0, 1.0)
    cos_ref[...] = jnp.cos(angles)
    sin_ref[...] = jnp.sin(angles) * sign

    def transpose(src, dst, j):
        part = src[:, 256 * j : 256 * (j + 1)].T
        for i in range(2):
            for h in range(2):
                b = 2 * j + i
                dst[h, b * 64 : (b + 1) * 64, :] = part[i * 128 + h * 64 : i * 128 + h * 64 + 64]

    to_mirror.wait_recv()
    ring_b = Ring(other_half)
    shared.append(weight(y * 2 + other_half, half, 64, mate))
    load_og.wait()
    load_as.wait()
    for j in range(4):
        transpose(og, og_t, j)
    ring_a.step(1)
    for j in range(4, 8):
        transpose(og, og_t, j)

    def put_z(dst, block, tile):
        for qr in range(4):
            zz = (block % 2) * 4 + qr
            yy = block // 2
            dst[zz, yy * 16 : yy * 16 + 16, :] = tile[qr * 16 : qr * 16 + 16]

    def out_term(h, ch):
        return dot(og_t[h, ch * 256 : (ch + 1) * 256, :], saved[...])

    for ch in range(4):
        part = out_term(1 - c, ch).astype(BF16)
        for i in range(4):
            put_z(gs_z, ch * 4 + i, part[i * 64 : i * 64 + 64])
    core_z = links.send(gs_z, gr_z, mate)
    ring_b.step(1)
    ring_a.step(2)
    for ch in range(4):
        part = out_term(c, ch)
        for i in range(4):
            put_z(s_z, ch * 4 + i, part[i * 64 : i * 64 + 64].astype(BF16))
    core_z.wait_recv()
    for k in range(8):
        s_z[k] = (s_z[k].astype(F32) + gr_z[k].astype(F32)).astype(BF16)
    first_z = [links.send(s_z.at[mod(z + d, 8)], r_z.at[d - 1], at_z(d)) for d in range(1, 8)]
    ring_b.step(2)
    load_hid.wait()
    for j in range(4):
        transpose(hid, hid_t, j)
    ring_a.step(3)
    for j in range(4, 8):
        transpose(hid, hid_t, j)
    ring_b.step(3)
    ring_a.step(4)
    ring_b.step(4)
    arrived(shared)

    proj[:, :512] = dot(hid[...], wbuf[:, :512])
    proj[:, 512:] = dot(og[...], wbuf[:, 512:])
    cosine, sines = cos_ref[...], sin_ref[...]

    def rotary(value):
        return value * cosine + pltpu.roll(value, HEAD // 2, 1) * sines

    def rotary_back(value):
        return value * cosine - pltpu.roll(value, HEAD // 2, 1) * sines

    keys = rotary(proj[:, 256:384]).astype(BF16)
    values = proj[:, 384:512].astype(BF16)
    row = lax.broadcasted_iota(jnp.int32, (ROWS, ROWS), 0)
    col = lax.broadcasted_iota(jnp.int32, (ROWS, ROWS), 1)
    allowed = col <= row
    end = jnp.int32(0)
    for i in range(4):
        end = end + doc_ref[0, i]
        allowed = allowed & ((row >= end) == (col >= end))
    scale = 1.0 / HEAD**0.5
    key_grad = jnp.zeros((ROWS, HEAD), F32)
    value_grad = jnp.zeros((ROWS, HEAD), F32)
    for h in range(2):
        lanes = slice(h * HEAD, (h + 1) * HEAD)
        query = rotary(proj[:, lanes]).astype(BF16)
        grad = proj[:, 512 + h * HEAD : 512 + (h + 1) * HEAD].astype(BF16)
        scores = dot(query, keys, ((1,), (1,))) * scale
        probs = jnp.where(allowed, jnp.exp(scores - lse_ref[:, h : h + 1]), 0.0)
        dprobs = dot(grad, values, ((1,), (1,)))
        delta = jnp.sum(
            grad.astype(F32) * saved[:, lanes].astype(F32), axis=1, keepdims=True
        )
        dscores = (probs * (dprobs - delta) * scale).astype(BF16)
        value_grad += dot(probs.astype(BF16), grad, ((0,), (0,)))
        key_grad += dot(dscores, query, ((0,), (0,)))
        dqkv[:, lanes] = rotary_back(dot(dscores, keys)).astype(BF16)
    dqkv[:, 256:384] = rotary_back(key_grad).astype(BF16)
    dqkv[:, 384:512] = value_grad.astype(BF16)

    def put_yx(dst_y, dst_x, block, tile):
        yy, side = block // 2, block % 2
        dst_y[yy, side * 64 : side * 64 + 64, :] = tile[:, :256]
        for qr in range(4):
            for ct in range(2):
                dst_x[qr * 2 + ct, block * 16 : block * 16 + 16, :] = tile[
                    qr * 16 : qr * 16 + 16, 256 + ct * 128 : 384 + ct * 128
                ]

    def qkv_term(h, ch):
        return dot(hid_t[h, ch * 256 : (ch + 1) * 256, :], dqkv[...])

    core_y, core_x = [], []
    for ch in range(4):
        part = qkv_term(1 - c, ch).astype(BF16)
        for i in range(4):
            put_yx(gs_y, gs_x, ch * 4 + i, part[i * 64 : i * 64 + 64])
        where = pl.ds(ch * 2, 2)
        core_y.append(links.send(gs_y.at[where], gr_y.at[where], mate))
        where = (slice(None), pl.ds(ch * 64, 64), slice(None))
        core_x.append(links.send(gs_x.at[where], gr_x.at[where], mate))
    for ch in range(4):
        part = qkv_term(c, ch).astype(BF16)
        for i in range(4):
            put_yx(s_y, s_x, ch * 4 + i, part[i * 64 : i * 64 + 64])
    arrived(core_y)
    for k in range(8):
        s_y[k] = (s_y[k].astype(F32) + gr_y[k].astype(F32)).astype(BF16)
    first_y = [links.send(s_y.at[mod(y + d, 8)], r_y.at[d - 1], at_y(d)) for d in range(1, 8)]
    arrived(core_x)
    for k in range(8):
        s_x[k] = (s_x[k].astype(F32) + gr_x[k].astype(F32)).astype(BF16)
    first_x = [links.send(s_x.at[mod(x + d, 8)], r_x.at[d - 1], at_x(d)) for d in range(1, 8)]

    def summed(own_part, parts):
        total = own_part.astype(F32)
        for i in range(7):
            total = total + parts[i].astype(F32)
        return total

    def in_order(parts):
        total = parts[0].astype(F32)
        for i in range(1, 8):
            total = total + parts[i].astype(F32)
        return total

    arrived(first_z)
    total = summed(s_z[z], r_z).astype(BF16)
    for k in range(8):
        s2_z[k] = total[k * 16 : k * 16 + 16]
    second_z = [links.send(s2_z.at[mod(y + d, 8)], r2_z.at[d - 1], at_y(d)) for d in range(1, 8)]

    for n in range(4):
        cols = slice(n * 512, (n + 1) * 512)
        igv[:, cols] = dot(dqkv[...], wbuf[cols, :512], ((1,), (1,))).astype(BF16)
    store_ig = pltpu.make_async_copy(igv, ig_hbm, local.at[5])
    store_ig.start()

    arrived(second_z)
    r3_z[x] = summed(s2_z[y], r2_z).astype(BF16)
    third_z = [links.send(r3_z.at[x], r3_z.at[x], at_x(d)) for d in range(1, 8)]

    arrived(first_y)
    total = summed(s_y[y], r_y).astype(BF16)
    for k in range(8):
        s2_y[k] = total[k * 16 : k * 16 + 16]
    second_y = [links.send(s2_y.at[mod(z + d, 8)], r2_y.at[d - 1], at_z(d)) for d in range(1, 8)]
    arrived(first_x)
    total = summed(s_x[x], r_x).astype(BF16)
    for k in range(8):
        s2_x[k] = total[k * 32 : k * 32 + 32]
    second_x = [links.send(s2_x.at[mod(y + d, 8)], r2_x.at[d - 1], at_y(d)) for d in range(1, 8)]

    mine = c * 4 + zl
    arrived(third_z)
    fa[mine, :, 256:512] = in_order(r3_z)

    arrived(second_y)
    r3_y[x] = summed(s2_y[z], r2_y).astype(BF16)
    third_y = [links.send(r3_y.at[x], r3_y.at[x], at_x(d)) for d in range(1, 8)]
    arrived(second_x)
    total = summed(s2_x[y], r2_x).astype(BF16)
    for k in range(2):
        s3_x[k] = total[k * 16 : k * 16 + 16]
    r3_x[z] = s3_x[zh]
    third_x = [
        links.send(s3_x.at[mod(z + d, 8) // 4], r3_x.at[z], at_z(d)) for d in range(1, 8)
    ]

    arrived(third_y)
    fa[mine, :, 0:256] = in_order(r3_y)
    spread = [
        links.send(fa.at[mine], fa.at[mine], at_zl(d, dc) if d else mate)
        for d in range(4)
        for dc in range(2)
        if d or dc
    ]
    arrived(third_x)
    tile = c * 8 + x
    fx[tile] = in_order(r3_x)
    spread += [
        links.send(fx.at[tile], fx.at[tile], at_x(d, dc) if d else mate)
        for d in range(8)
        for dc in range(2)
        if d or dc
    ]
    arrived(spread)
    for i in range(8):
        grads_ref[i * 16 : i * 16 + 16, 0:256] = fa[i, :, 0:256]
        grads_ref[i * 16 : i * 16 + 16, 512:768] = fa[i, :, 256:512]
        for ct in range(2):
            at = (i // 4) * 8 + (i % 4) * 2 + ct
            grads_ref[i * 16 : i * 16 + 16, 256 + ct * 128 : 384 + ct * 128] = fx[at]
    whole = grads_ref[...]
    square = (whole * whole).reshape(16, 8, 768).sum(axis=0)
    tile_sum = square[:, 0:128]
    for i in range(1, 6):
        tile_sum = tile_sum + square[:, i * 128 : i * 128 + 128]
    nz[0] = tile_sum
    across = links.send(nz.at[0], nz.at[1], mirror)
    across.wait_recv()
    ny[y] = nz[0] + nz[1]
    along = [links.send(ny.at[y], ny.at[y], at_y(d)) for d in range(1, 8)]
    arrived(along)
    total = ny[0]
    for i in range(1, 8):
        total = total + ny[i]
    norm_ref[...] = total
    links.finish()
    store_ig.wait()
    assert links.used <= SEMS


def body(hidden_in, out_grad, attn_saved, row_lse, w_qkv, w_out_t, doc_lengths, seq_start):
    power = np.arange(HEAD // 2, dtype=np.float64) * 2.0 / HEAD
    inverse = np.tile(1000000.0 ** (-power), 2).astype(np.float32)[None, :]
    smem = pl.BlockSpec(memory_space=pltpu.SMEM)
    vmem = pl.BlockSpec(memory_space=pltpu.VMEM)
    hbm = pl.BlockSpec(memory_space=pl.ANY)
    half = (8, 128, 256)
    tall = (8, 256, 128)

    def bf(*shape):
        return pltpu.VMEM(shape, BF16)

    def f32(*shape):
        return pltpu.VMEM(shape, F32)

    input_grad, grads, tiles = pl.pallas_call(
        kernel,
        out_shape=(
            jax.ShapeDtypeStruct((ROWS, D), BF16),
            jax.ShapeDtypeStruct((128, 768), F32),
            jax.ShapeDtypeStruct((8, 128), F32),
        ),
        in_specs=[smem, smem, vmem, vmem, hbm, hbm, hbm, hbm, hbm],
        out_specs=(hbm, vmem, vmem),
        scratch_shapes=[
            bf(ROWS, D),
            bf(ROWS, D),
            bf(ROWS, 256),
            bf(D, 768),
            bf(2, 1024, 256),
            bf(2, 1024, 256),
            f32(ROWS, 768),
            f32(ROWS, HEAD),
            f32(ROWS, HEAD),
            bf(ROWS, 512),
            bf(ROWS, D),
            bf(*half),
            bf(*tall),
            bf(*half),
            bf(*half),
            bf(*tall),
            bf(*half),
            bf(*half),
            bf(*tall),
            bf(*half),
            bf(7, 128, 256),
            bf(7, 256, 128),
            bf(7, 128, 256),
            bf(8, 16, 256),
            bf(8, 32, 128),
            bf(8, 16, 256),
            bf(7, 16, 256),
            bf(7, 32, 128),
            bf(7, 16, 256),
            bf(8, 16, 256),
            bf(2, 16, 128),
            bf(8, 16, 128),
            bf(8, 16, 256),
            f32(8, 16, 512),
            f32(16, 16, 128),
            f32(2, 8, 128),
            f32(8, 8, 128),
            pltpu.SemaphoreType.DMA((SEMS,)),
            pltpu.SemaphoreType.DMA((6,)),
        ],
        compiler_params=pltpu.CompilerParams(collective_id=0, has_side_effects=True),
        name="attention_backward",
    )(
        seq_start,
        doc_lengths,
        jnp.asarray(inverse),
        row_lse,
        hidden_in,
        out_grad,
        attn_saved,
        w_qkv,
        w_out_t,
    )
    norm_sq = jnp.sum(tiles)
    grad_update = grads * lax.rsqrt(norm_sq / (D * 768) + 1e-06)
    return (input_grad, grad_update, jnp.sqrt(norm_sq))


def solution(mesh):
    split = Mesh(mesh.devices.reshape(8, 2, 4, 8, 2), AXES)
    tokens = P(FSDP_REP, None)
    in_specs = (tokens, tokens, tokens, tokens, P(FSDP, None), P(FSDP, None), tokens, P(FSDP_REP))
    out_specs = (tokens, P(FSDP, None), P())
    return jax.shard_map(body, mesh=split, in_specs=in_specs, out_specs=out_specs, check_vma=False)
```

time: 527 us -> 107 us (0.20)
  waiting for transfers between devices: 427 us -> 0 us
  Pallas kernels: 0 us -> 95.8 us
  blocking collectives: 26.8 us -> 0 us
  local copies, waits for them, and re-layouts: 27.2 us -> 3.78 us
  between operations: 17.2 us -> 3.8 us
  matrix products: 11.7 us -> 0 us
  starting transfers between devices: 6.96 us -> 0 us
  other arithmetic: 8.77 us -> 3.05 us
    unnamed x4 -> x0, waiting for transfers between devices: 263 us -> none
    all_gather x1 -> x0, waiting for transfers between devices: 133 us -> none  [sent_together(): whole, at, outs = (lax.all_gather(both, axis, axis=dim, tiled=True), 0, [])]
    pallas_call x0 -> x1, Pallas kernels: none -> 95.8 us  [body(): pl.pallas_call(kernel, out_shape=(jax.ShapeDtypeStruct((ROWS, D), BF16),...]
    all_to_all x1 -> x0, blocking collectives: 26.8 us -> none  [copy_for_each(): return lax.all_to_all(copies, axis, split_axis=0, concat_axis=0, tiled=True)]
    reduce_scatter x1 -> x0, waiting for transfers between devices: 24 us -> none  [summed_rows_2(): tiles = lax.psum_scatter(tiles, core, scatter_dimension=0, tiled=True)]
    reshape x4 -> x0, local copies, waits for them, and re-layouts: 20.3 us -> none  [the longest x3 20.2 us: summed_rows_2(): tiles = tiles.reshape(*sizes, *inside).swapaxes(0, 1).reshape(-1, *inside)]
    dot_general x15 -> x0, matrix products: 11.7 us -> none  [the longest x5 4.23 us: contract_cols(): lax.dot_general(left, right, (((1,), (1,)), ((), ())), preferred_element_...]
    all_to_all x1 -> x0, waiting for transfers between devices: 7.89 us -> none  [copy_for_each(): return lax.all_to_all(copies, axis, split_axis=0, concat_axis=0, tiled=True)]
  transfers between devices with their start and end apart: 4 -> 0, of which waited for: 4 -> 0; matrix products, arithmetic and copies ran while one was open for 2% -> 0% of each run, Pallas kernels for 0% -> 0%
where the time goes in v1:
time: 107 us; the launch traced here: 106 us
  Pallas kernels  95.8 us (90%)
  between operations  3.8 us (4%)
  local copies, waits for them, and re-layouts  3.78 us (4%)
  other arithmetic  3.05 us (3%)
    pallas_call x1, Pallas kernels, body(): pl.pallas_call(kernel, out_shape=(jax.ShapeDtypeStruct((ROWS, D), BF16),...  95.8 us
    unnamed x2, local copies, waits for them, and re-layouts  3.78 us

profile of v1, /device:TPU:1, one launch (start us, length us, event | category | flops | bytes accessed | tf_op | source)
XLA Modules:
  0.0 106.4 jit_solution(887371713899689709)
XLA Ops:
  0.6 1.5 %copy.12.lse_ref = f32[256,2]{1,0:T(8,128)} copy(f32[256,2]{0,1:T(2,128)} %param.12) | data formatting | bytes 4096 | tf_op args[3]
  2.8 95.8 %attention_backward.1 = (bf16[256,2048]{1,0:T(8,128)(2,1)}, f32[128,768]{1,0:T(8,128)}, f32[8,128]{1,0:T(8,128)}) custom-call(s32[1]{0:T(128)S(6)} %copy.14.start_ref, s32[1,4]{1,0:T(1,128)} %doc_ref.1, f32[1,128]{1,0:T(1,128)} %constant.9.clone.inv_ref, f32[256,2]{1,0:T(8,128)} %copy.12.lse_ref, bf16[256,2048]{1,0:T(8,128)(2,1)} %hid_hbm.1, ...), custom_call_target="tpu_custom_call" | custom-call | tf_op jit(solution)/shard_map/attention_backward/pallas_call | solution.py:448
  98.6 1.3 %reduce_sum.9 = f32[]{:T(128)} reduce(f32[8,128]{1,0:T(8,128)} %get-tuple-element.8, f32[]{:T(128)} %constant.2.clone.1), dimensions={0,1}, to_apply=%region_0.0 | reduce | flops 1023 | bytes 4104 | tf_op jit(solution)/shard_map/reduce_sum | solution.py:511
  100.5 1.8 %broadcast_multiply_fusion = f32[128,768]{1,0:T(8,128)} fusion(f32[128,768]{1,0:T(8,128)} %get-tuple-element.7, f32[]{:T(128)S(6)} %rsqrt.3), kind=kLoop, calls=%fused_computation | loop fusion | flops 98304 | bytes 786436 | tf_op jit(solution)/shard_map/mul | solution.py:512
  103.0 2.3 %copy.15 = bf16[256,2048]{1,0:T(8,128)(2,1)} copy(bf16[256,2048]{1,0:T(8,128)(2,1)} %get-tuple-element.12) | data formatting | bytes 2097152

commit v2 on v1

--- a/solution.py
+++ b/solution.py
@@ -65,7 +65,7 @@
     as_hbm,
     wq_hbm,
     wo_hbm,
-    ig_hbm,
+    ig_ref,
     grads_ref,
     norm_ref,
     hid,
@@ -75,10 +75,10 @@
     hid_t,
     og_t,
     proj,
+    lse,
     cos_ref,
     sin_ref,
     dqkv,
-    igv,
     gs_y,
     gs_x,
     gs_z,
@@ -101,9 +101,12 @@
     s3_x,
     r3_x,
     r3_z,
-    fa,
+    far_y,
+    far_x,
+    far_z,
+    fy,
+    fz,
     fx,
-    nz,
     ny,
     sems,
     local,
@@ -127,6 +130,9 @@
         there = mod(z + d, 8)
         return (y, there // 4, lax.rem(there, 4), x, c)
 
+    def across(d):
+        return (mod(y + d, 8), 1 - zh, 3 - zl, x, c)
+
     def at_zl(d, dc):
         return (y, zh, mod(zl + d, 4), x, mod(c + dc, 2))
 
@@ -135,6 +141,7 @@
     peers += [at_x(d, dc) for d in range(1, 8) for dc in range(2)]
     peers += [at_z(d) for d in range(1, 8)]
     peers += [at_zl(d, 1) for d in range(1, 4)]
+    peers += [across(d) for d in range(1, 8)]
     barrier = pltpu.get_barrier_semaphore()
     extra = len(peers)
     for peer in peers:
@@ -201,6 +208,8 @@
     positions = (start_ref[0] + lax.broadcasted_iota(jnp.int32, (ROWS, HEAD), 0)).astype(F32)
     angles = positions * inv_ref[...]
     sign = jnp.where(lax.broadcasted_iota(jnp.int32, (ROWS, HEAD), 1) < HEAD // 2, -1.0, 1.0)
+    for h in range(2):
+        lse[h] = jnp.broadcast_to(lse_ref[h : h + 1, :], (HEAD, ROWS)).T
     cos_ref[...] = jnp.cos(angles)
     sin_ref[...] = jnp.sin(angles) * sign
 
@@ -221,6 +230,41 @@
     ring_a.step(1)
     for j in range(4, 8):
         transpose(og, og_t, j)
+
+    sign_c = 1 - 2 * c
+
+    class First:
+        def __init__(self, chunks, parts, relay, me, at):
+            self.chunks, self.parts, self.relay, self.me, self.at = chunks, parts, relay, me, at
+            self.far = links.send(chunks.at[mod(me + 4, 8)], relay, at(sign_c))
+            self.sent = [self.go(i, d) for i, d in enumerate((-3, 2, -2, 1, -1))]
+
+        def go(self, i, d):
+            there = mod(self.me + sign_c * d, 8)
+            return links.send(self.chunks.at[there], self.parts.at[i], self.at(sign_c * d))
+
+        def pass_on(self):
+            self.far.wait_recv()
+            there = mod(self.me + sign_c * 3, 8)
+            both = self.chunks[there].astype(F32) + self.relay[...].astype(F32)
+            self.chunks[there] = both.astype(BF16)
+            self.sent.append(self.go(5, 3))
+
+        def total(self):
+            arrived(self.sent)
+            return summed(self.chunks[self.me], self.parts, 6).astype(BF16)
+
+    def summed(own_part, parts, count):
+        total = own_part.astype(F32)
+        for i in range(count):
+            total = total + parts[i].astype(F32)
+        return total
+
+    def in_order(parts):
+        total = parts[0].astype(F32)
+        for i in range(1, 8):
+            total = total + parts[i].astype(F32)
+        return total
 
     def put_z(dst, block, tile):
         for qr in range(4):
@@ -245,8 +289,9 @@
     core_z.wait_recv()
     for k in range(8):
         s_z[k] = (s_z[k].astype(F32) + gr_z[k].astype(F32)).astype(BF16)
-    first_z = [links.send(s_z.at[mod(z + d, 8)], r_z.at[d - 1], at_z(d)) for d in range(1, 8)]
+    first_z = First(s_z, r_z, far_z, z, at_z)
     ring_b.step(2)
+    first_z.pass_on()
     load_hid.wait()
     for j in range(4):
         transpose(hid, hid_t, j)
@@ -285,7 +330,7 @@
         query = rotary(proj[:, lanes]).astype(BF16)
         grad = proj[:, 512 + h * HEAD : 512 + (h + 1) * HEAD].astype(BF16)
         scores = dot(query, keys, ((1,), (1,))) * scale
-        probs = jnp.where(allowed, jnp.exp(scores - lse_ref[:, h : h + 1]), 0.0)
+        probs = jnp.where(allowed, jnp.exp(scores - lse[h, :, 0:1]), 0.0)
         dprobs = dot(grad, values, ((1,), (1,)))
         delta = jnp.sum(
             grad.astype(F32) * saved[:, lanes].astype(F32), axis=1, keepdims=True
@@ -322,63 +367,56 @@
         part = qkv_term(c, ch).astype(BF16)
         for i in range(4):
             put_yx(s_y, s_x, ch * 4 + i, part[i * 64 : i * 64 + 64])
+    total = first_z.total()
+    for k in range(8):
+        s2_z[k] = total[k * 16 : k * 16 + 16]
+    second_z = [links.send(s2_z.at[mod(y + d, 8)], r2_z.at[d - 1], at_y(d)) for d in range(1, 8)]
     arrived(core_y)
     for k in range(8):
         s_y[k] = (s_y[k].astype(F32) + gr_y[k].astype(F32)).astype(BF16)
-    first_y = [links.send(s_y.at[mod(y + d, 8)], r_y.at[d - 1], at_y(d)) for d in range(1, 8)]
+    first_y = First(s_y, r_y, far_y, y, at_y)
     arrived(core_x)
     for k in range(8):
         s_x[k] = (s_x[k].astype(F32) + gr_x[k].astype(F32)).astype(BF16)
-    first_x = [links.send(s_x.at[mod(x + d, 8)], r_x.at[d - 1], at_x(d)) for d in range(1, 8)]
-
-    def summed(own_part, parts):
-        total = own_part.astype(F32)
-        for i in range(7):
-            total = total + parts[i].astype(F32)
-        return total
-
-    def in_order(parts):
-        total = parts[0].astype(F32)
-        for i in range(1, 8):
-            total = total + parts[i].astype(F32)
-        return total
-
-    arrived(first_z)
-    total = summed(s_z[z], r_z).astype(BF16)
-    for k in range(8):
-        s2_z[k] = total[k * 16 : k * 16 + 16]
-    second_z = [links.send(s2_z.at[mod(y + d, 8)], r2_z.at[d - 1], at_y(d)) for d in range(1, 8)]
+    first_x = First(s_x, r_x, far_x, x, at_x)
 
     for n in range(4):
         cols = slice(n * 512, (n + 1) * 512)
-        igv[:, cols] = dot(dqkv[...], wbuf[cols, :512], ((1,), (1,))).astype(BF16)
-    store_ig = pltpu.make_async_copy(igv, ig_hbm, local.at[5])
-    store_ig.start()
+        ig_ref[:, cols] = dot(dqkv[...], wbuf[cols, :512], ((1,), (1,))).astype(BF16)
+    first_y.pass_on()
+    first_x.pass_on()
 
     arrived(second_z)
-    r3_z[x] = summed(s2_z[y], r2_z).astype(BF16)
+    r3_z[x] = summed(s2_z[y], r2_z, 7).astype(BF16)
     third_z = [links.send(r3_z.at[x], r3_z.at[x], at_x(d)) for d in range(1, 8)]
 
-    arrived(first_y)
-    total = summed(s_y[y], r_y).astype(BF16)
+    total = first_y.total()
     for k in range(8):
         s2_y[k] = total[k * 16 : k * 16 + 16]
     second_y = [links.send(s2_y.at[mod(z + d, 8)], r2_y.at[d - 1], at_z(d)) for d in range(1, 8)]
-    arrived(first_x)
-    total = summed(s_x[x], r_x).astype(BF16)
+    total = first_x.total()
     for k in range(8):
         s2_x[k] = total[k * 32 : k * 32 + 32]
     second_x = [links.send(s2_x.at[mod(y + d, 8)], r2_x.at[d - 1], at_y(d)) for d in range(1, 8)]
 
+    def spread_zl(pieces):
+        return [
+            links.send(pieces.at[mine], pieces.at[mine], at_zl(d, dc) if d else mate)
+            for d in range(4)
+            for dc in range(2)
+            if d or dc
+        ]
+
     mine = c * 4 + zl
     arrived(third_z)
-    fa[mine, :, 256:512] = in_order(r3_z)
+    fz[mine] = in_order(r3_z).astype(BF16)
+    spread = spread_zl(fz)
 
     arrived(second_y)
-    r3_y[x] = summed(s2_y[z], r2_y).astype(BF16)
+    r3_y[x] = summed(s2_y[z], r2_y, 7).astype(BF16)
     third_y = [links.send(r3_y.at[x], r3_y.at[x], at_x(d)) for d in range(1, 8)]
     arrived(second_x)
-    total = summed(s2_x[y], r2_x).astype(BF16)
+    total = summed(s2_x[y], r2_x, 7).astype(BF16)
     for k in range(2):
         s3_x[k] = total[k * 16 : k * 16 + 16]
     r3_x[z] = s3_x[zh]
@@ -387,16 +425,11 @@
     ]
 
     arrived(third_y)
-    fa[mine, :, 0:256] = in_order(r3_y)
-    spread = [
-        links.send(fa.at[mine], fa.at[mine], at_zl(d, dc) if d else mate)
-        for d in range(4)
-        for dc in range(2)
-        if d or dc
-    ]
+    fy[mine] = in_order(r3_y).astype(BF16)
+    spread += spread_zl(fy)
     arrived(third_x)
     tile = c * 8 + x
-    fx[tile] = in_order(r3_x)
+    fx[tile] = in_order(r3_x).astype(BF16)
     spread += [
         links.send(fx.at[tile], fx.at[tile], at_x(d, dc) if d else mate)
         for d in range(8)
@@ -405,29 +438,35 @@
     ]
     arrived(spread)
     for i in range(8):
-        grads_ref[i * 16 : i * 16 + 16, 0:256] = fa[i, :, 0:256]
-        grads_ref[i * 16 : i * 16 + 16, 512:768] = fa[i, :, 256:512]
+        grads_ref[i * 16 : i * 16 + 16, 0:256] = fy[i].astype(F32)
+        grads_ref[i * 16 : i * 16 + 16, 512:768] = fz[i].astype(F32)
         for ct in range(2):
             at = (i // 4) * 8 + (i % 4) * 2 + ct
-            grads_ref[i * 16 : i * 16 + 16, 256 + ct * 128 : 384 + ct * 128] = fx[at]
+            grads_ref[i * 16 : i * 16 + 16, 256 + ct * 128 : 384 + ct * 128] = fx[at].astype(F32)
     whole = grads_ref[...]
     square = (whole * whole).reshape(16, 8, 768).sum(axis=0)
     tile_sum = square[:, 0:128]
     for i in range(1, 6):
         tile_sum = tile_sum + square[:, i * 128 : i * 128 + 128]
-    nz[0] = tile_sum
-    across = links.send(nz.at[0], nz.at[1], mirror)
-    across.wait_recv()
-    ny[y] = nz[0] + nz[1]
-    along = [links.send(ny.at[y], ny.at[y], at_y(d)) for d in range(1, 8)]
+    ny[own] = tile_sum
+    along = [links.send(ny.at[own], ny.at[own], at_y(d)) for d in range(1, 8)]
+    along += [links.send(ny.at[own], ny.at[own], across(d)) for d in range(8)]
     arrived(along)
     total = ny[0]
-    for i in range(1, 8):
+    for i in range(1, 16):
         total = total + ny[i]
     norm_ref[...] = total
     links.finish()
-    store_ig.wait()
     assert links.used <= SEMS
+
+
+def finish(ig_ref, grads_ref, tiles_ref, ig_out, update_ref, norm_ref, sem):
+    store = pltpu.make_async_copy(ig_ref, ig_out, sem)
+    store.start()
+    norm_sq = jnp.sum(jnp.sum(tiles_ref[...], axis=0, keepdims=True), axis=1, keepdims=True)
+    update_ref[...] = grads_ref[...] * lax.rsqrt(norm_sq / (D * 768) + 1e-06)
+    norm_ref[...] = jnp.sqrt(norm_sq)
+    store.wait()
 
 
 def body(hidden_in, out_grad, attn_saved, row_lse, w_qkv, w_out_t, doc_lengths, seq_start):
@@ -447,13 +486,9 @@
 
     input_grad, grads, tiles = pl.pallas_call(
         kernel,
-        out_shape=(
-            jax.ShapeDtypeStruct((ROWS, D), BF16),
-            jax.ShapeDtypeStruct((128, 768), F32),
-            jax.ShapeDtypeStruct((8, 128), F32),
-        ),
+        out_shape=(bf(ROWS, D), f32(128, 768), f32(8, 128)),
         in_specs=[smem, smem, vmem, vmem, hbm, hbm, hbm, hbm, hbm],
-        out_specs=(hbm, vmem, vmem),
+        out_specs=(vmem, vmem, vmem),
         scratch_shapes=[
             bf(ROWS, D),
             bf(ROWS, D),
@@ -462,10 +497,10 @@
             bf(2, 1024, 256),
             bf(2, 1024, 256),
             f32(ROWS, 768),
+            f32(2, ROWS, HEAD),
             f32(ROWS, HEAD),
             f32(ROWS, HEAD),
             bf(ROWS, 512),
-            bf(ROWS, D),
             bf(*half),
             bf(*tall),
             bf(*half),
@@ -475,9 +510,9 @@
             bf(*half),
             bf(*tall),
             bf(*half),
-            bf(7, 128, 256),
-            bf(7, 256, 128),
-            bf(7, 128, 256),
+            bf(6, 128, 256),
+            bf(6, 256, 128),
+            bf(6, 128, 256),
             bf(8, 16, 256),
             bf(8, 32, 128),
             bf(8, 16, 256),
@@ -488,12 +523,15 @@
             bf(2, 16, 128),
             bf(8, 16, 128),
             bf(8, 16, 256),
-            f32(8, 16, 512),
-            f32(16, 16, 128),
-            f32(2, 8, 128),
-            f32(8, 8, 128),
+            bf(128, 256),
+            bf(256, 128),
+            bf(128, 256),
+            bf(8, 16, 256),
+            bf(8, 16, 256),
+            bf(16, 16, 128),
+            f32(16, 8, 128),
             pltpu.SemaphoreType.DMA((SEMS,)),
-            pltpu.SemaphoreType.DMA((6,)),
+            pltpu.SemaphoreType.DMA((5,)),
         ],
         compiler_params=pltpu.CompilerParams(collective_id=0, has_side_effects=True),
         name="attention_backward",
@@ -501,16 +539,27 @@
         seq_start,
         doc_lengths,
         jnp.asarray(inverse),
-        row_lse,
+        row_lse.T,
         hidden_in,
         out_grad,
         attn_saved,
         w_qkv,
         w_out_t,
     )
-    norm_sq = jnp.sum(tiles)
-    grad_update = grads * lax.rsqrt(norm_sq / (D * 768) + 1e-06)
-    return (input_grad, grad_update, jnp.sqrt(norm_sq))
+    input_grad, grad_update, norm = pl.pallas_call(
+        finish,
+        out_shape=(
+            jax.ShapeDtypeStruct((ROWS, D), BF16),
+            jax.ShapeDtypeStruct((128, 768), F32),
+            jax.ShapeDtypeStruct((1, 1), F32),
+        ),
+        in_specs=[vmem] * 3,
+        out_specs=(hbm, vmem, vmem),
+        scratch_shapes=[pltpu.SemaphoreType.DMA],
+        compiler_params=pltpu.CompilerParams(vmem_limit_bytes=8 * 2**20),
+        name="scaled_outputs",
+    )(input_grad, grads, tiles)
+    return (input_grad, grad_update, norm[0, 0])
 
 
 def solution(mesh):

time: 107 us -> 94.6 us (0.88)
  local copies, waits for them, and re-layouts: 3.78 us -> 0 us
  other arithmetic: 3.05 us -> 0 us
  Pallas kernels: 95.8 us -> 93.1 us
  between operations: 3.8 us -> 1.29 us
    unnamed x2 -> x0, local copies, waits for them, and re-layouts: 3.78 us -> none
    pallas_call x1 -> x2, Pallas kernels: 95.8 us -> 93.1 us  [the longest x1 91.4 us: body(): pl.pallas_call(kernel, out_shape=(bf(ROWS, D), f32(128, 768), f32(8, 128)...]
    mul x1 -> x0, other arithmetic: 1.77 us -> none  [body(): grad_update = grads * lax.rsqrt(norm_sq / (D * 768) + 1e-06)]
    reduce_sum x1 -> x0, other arithmetic: 1.28 us -> none  [body(): norm_sq = jnp.sum(tiles)]
where the time goes in v2:
time: 94.6 us; the launch traced here: 94.4 us
  Pallas kernels  93.1 us (98%)
  between operations  1.29 us (1%)
    pallas_call x1, Pallas kernels, body(): pl.pallas_call(kernel, out_shape=(bf(ROWS, D), f32(128, 768), f32(8, 128)...  91.4 us

profile of v2, /device:TPU:1, one launch (start us, length us, event | category | flops | bytes accessed | tf_op | source)
XLA Modules:
  0.0 94.4 jit_solution(9995264545379774848)
XLA Ops:
  1.3 91.4 %attention_backward.1 = (bf16[256,2048]{1,0:T(8,128)(2,1)S(1)}, f32[128,768]{1,0:T(8,128)S(1)}, f32[8,128]{1,0:T(8,128)S(1)}) custom-call(s32[1]{0:T(128)S(6)} %copy.12.start_ref, s32[1,4]{1,0:T(1,128)} %doc_ref.1, f32[1,128]{1,0:T(1,128)} %constant.2.clone.inv_ref, f32[2,256]{1,0:T(2,128)} %bitcast.2, bf16[256,2048]{1,0:T(8,128)(2,1)} %hid_hbm.1, ...), custom_call_target="tpu_custom_call" | custom-call | tf_op jit(solution)/shard_map/attention_backward/pallas_call | solution.py:487
  92.6 1.7 %scaled_outputs.1 = (bf16[256,2048]{1,0:T(8,128)(2,1)}, f32[128,768]{1,0:T(8,128)}, f32[1,1]{1,0:T(1,128)}) custom-call(bf16[256,2048]{1,0:T(8,128)(2,1)S(1)} %get-tuple-element.9.ig_ref, f32[128,768]{1,0:T(8,128)S(1)} %get-tuple-element.10.grads_ref, f32[8,128]{1,0:T(8,128)S(1)} %get-tuple-element.11.tiles_ref), custom_call_target="tpu_custom_call" | custom-call | tf_op jit(solution)/shard_map/scaled_outputs/pallas_call | solution.py:549

commit v3 on v2

--- a/solution.py
+++ b/solution.py
@@ -15,7 +15,7 @@
 FSDP_REP = AXES
 F32 = jnp.float32
 BF16 = jnp.bfloat16
-SEMS = 360
+SEMS = 540
 
 
 def mod(value, size):
@@ -107,9 +107,12 @@
     fy,
     fz,
     fx,
+    nz,
+    nx,
     ny,
     sems,
     local,
+    chain,
 ):
     y = lax.axis_index(AXES[0])
     zh = lax.axis_index(AXES[1])
@@ -126,29 +129,15 @@
     def at_x(d, dc=0):
         return (y, zh, zl, mod(x + d, 8), mod(c + dc, 2))
 
-    def at_z(d):
+    def at_z(d, dc=0):
         there = mod(z + d, 8)
-        return (y, there // 4, lax.rem(there, 4), x, c)
-
-    def across(d):
-        return (mod(y + d, 8), 1 - zh, 3 - zl, x, c)
+        return (y, there // 4, lax.rem(there, 4), x, mod(c + dc, 2))
 
     def at_zl(d, dc):
         return (y, zh, mod(zl + d, 4), x, mod(c + dc, 2))
 
-    peers = [mate]
-    peers += [at_y(d) for d in range(1, 8)]
-    peers += [at_x(d, dc) for d in range(1, 8) for dc in range(2)]
-    peers += [at_z(d) for d in range(1, 8)]
-    peers += [at_zl(d, 1) for d in range(1, 4)]
-    peers += [across(d) for d in range(1, 8)]
-    barrier = pltpu.get_barrier_semaphore()
-    extra = len(peers)
-    for peer in peers:
-        pl.semaphore_signal(barrier, inc=1, device_id=peer, device_id_type=pl.DeviceIdType.MESH)
-
     def rows_of(block, first, count):
-        return pl.ds(pl.multiple_of(block * 128 + first, 32), count)
+        return pl.ds(pl.multiple_of(block * 128 + first, 16), count)
 
     own = y * 2 + zh
     own_rows = rows_of(own, 0, 128)
@@ -159,9 +148,30 @@
     load_hid = pltpu.make_async_copy(hid_hbm, hid, local.at[4])
     for copy in (load_wq, load_wo, load_og, load_as, load_hid):
         copy.start()
+    near = [mate, mirror]
+    for at in (at_y, at_x, at_z):
+        near += [at(1), at(-1)]
+    barrier = pltpu.get_barrier_semaphore()
+
+    def tell(sem, device):
+        pl.semaphore_signal(sem, inc=1, device_id=device, device_id_type=pl.DeviceIdType.MESH)
+
+    for peer in near:
+        tell(barrier, peer)
+
     load_wq.wait()
     load_wo.wait()
-    pl.semaphore_wait(barrier, extra)
+    pl.semaphore_wait(barrier, len(near))
+
+    def hear(step):
+        for i in range(4):
+            pl.semaphore_wait(chain.at[step, i], 1)
+
+    def pass_word(step):
+        for i, device in enumerate((at_x(1), at_x(-1), at_z(1), at_z(-1))):
+            tell(chain.at[step, i], device)
+
+    pass_word(0)
 
     links = Links(sems)
 
@@ -169,41 +179,49 @@
         ref = wbuf.at[rows_of(block, first, count), :]
         return links.send(ref, ref, device)
 
-    half = c * 64
-    other_half = 1 - zh
-    to_mirror = weight(own, half, 64, mirror)
-    up, down = at_y(1), at_y(-1)
+    color = lax.rem(x, 2)
+    base, other_base = color * 64 + c * 32, (1 - color) * 64 + c * 32
+    along_y = (at_y(1), at_y(-1))
+    along_x = (at_x(1), at_x(-1))
     shared = []
 
     class Ring:
         def __init__(self, zside):
-            self.zside = zside
-            self.sent = [self.pass_on(0)]
+            self.zside, self.beside = zside, {0: []}
+            self.sent = {(w, u): self.piece(0, u, along_y[w]) for u in range(2) for w in range(2)}
 
         def block(self, d):
             return mod(y + d, 8) * 2 + self.zside
 
-        def pass_on(self, s):
-            if s < 3:
-                return (
-                    weight(self.block(-s), half, 64, up),
-                    weight(self.block(s), half, 64, down),
-                )
-            return (
-                weight(self.block(-3), half, 32, up),
-                weight(self.block(3), half + 32, 32, down),
-            )
+        def piece(self, d, u, device):
+            return weight(self.block(d), base + 16 * u, 16, device)
+
+        def hand_over(self, d, u, s):
+            self.beside[s].append(self.piece(d, u, along_x[u]))
+
+        def to_mate(self, d, first):
+            shared.append(weight(self.block(d), first, 32, mate))
 
         def step(self, s):
-            arrived(self.sent[-1])
-            if s < 4:
-                self.sent.append(self.pass_on(s))
-                shared.append(weight(self.block(-s), half, 64, mate))
-                shared.append(weight(self.block(s), half, 64, mate))
-            else:
-                shared.append(weight(self.block(4), half, 64, mate))
+            before, self.sent, self.beside[s] = self.sent, {}, []
+            for (w, u), copy in before.items():
+                copy.wait_recv()
+                d = s if w else -s
+                if s < 3 or (s == 3 and u == w):
+                    self.sent[w, u] = self.piece(d, u, along_y[w])
+                self.hand_over(d, u, s)
+            self.mate_rows(s, base)
+
+        def mate_rows(self, s, first):
+            for d in {0: (0,), 4: (4,)}.get(s, (-s, s)):
+                self.to_mate(d, first)
+
+        def collect(self, s):
+            arrived(self.beside[s])
+            self.mate_rows(s, other_base)
 
     ring_a = Ring(zh)
+    to_mirror = [weight(own, base + 16 * u, 16, mirror) for u in range(2)]
 
     positions = (start_ref[0] + lax.broadcasted_iota(jnp.int32, (ROWS, HEAD), 0)).astype(F32)
     angles = positions * inv_ref[...]
@@ -220,16 +238,21 @@
                 b = 2 * j + i
                 dst[h, b * 64 : (b + 1) * 64, :] = part[i * 128 + h * 64 : i * 128 + h * 64 + 64]
 
-    to_mirror.wait_recv()
-    ring_b = Ring(other_half)
-    shared.append(weight(y * 2 + other_half, half, 64, mate))
+    ring_a.step(1)
+    hear(0)
+    pass_word(1)
     load_og.wait()
     load_as.wait()
-    for j in range(4):
+    for j in range(8):
         transpose(og, og_t, j)
-    ring_a.step(1)
-    for j in range(4, 8):
-        transpose(og, og_t, j)
+    arrived(to_mirror)
+    ring_b = Ring(1 - zh)
+    for u in range(2):
+        ring_b.hand_over(0, u, 0)
+    ring_b.mate_rows(0, base)
+    ring_a.step(2)
+    hear(1)
+    pass_word(2)
 
     sign_c = 1 - 2 * c
 
@@ -280,8 +303,10 @@
         for i in range(4):
             put_z(gs_z, ch * 4 + i, part[i * 64 : i * 64 + 64])
     core_z = links.send(gs_z, gr_z, mate)
+    ring_a.collect(1)
+    ring_a.step(3)
     ring_b.step(1)
-    ring_a.step(2)
+    hear(2)
     for ch in range(4):
         part = out_term(c, ch)
         for i in range(4):
@@ -290,17 +315,24 @@
     for k in range(8):
         s_z[k] = (s_z[k].astype(F32) + gr_z[k].astype(F32)).astype(BF16)
     first_z = First(s_z, r_z, far_z, z, at_z)
+    ring_a.collect(2)
+    ring_b.collect(0)
+    ring_a.step(4)
     ring_b.step(2)
-    first_z.pass_on()
     load_hid.wait()
     for j in range(4):
         transpose(hid, hid_t, j)
-    ring_a.step(3)
+    ring_a.collect(3)
+    ring_b.collect(1)
+    ring_b.step(3)
+    first_z.pass_on()
     for j in range(4, 8):
         transpose(hid, hid_t, j)
-    ring_b.step(3)
-    ring_a.step(4)
+    ring_a.collect(4)
+    ring_b.collect(2)
     ring_b.step(4)
+    ring_b.collect(3)
+    ring_b.collect(4)
     arrived(shared)
 
     proj[:, :512] = dot(hid[...], wbuf[:, :512])
@@ -342,42 +374,43 @@
     dqkv[:, 256:384] = rotary_back(key_grad).astype(BF16)
     dqkv[:, 384:512] = value_grad.astype(BF16)
 
-    def put_yx(dst_y, dst_x, block, tile):
-        yy, side = block // 2, block % 2
-        dst_y[yy, side * 64 : side * 64 + 64, :] = tile[:, :256]
-        for qr in range(4):
-            for ct in range(2):
-                dst_x[qr * 2 + ct, block * 16 : block * 16 + 16, :] = tile[
-                    qr * 16 : qr * 16 + 16, 256 + ct * 128 : 384 + ct * 128
-                ]
-
-    def qkv_term(h, ch):
-        return dot(hid_t[h, ch * 256 : (ch + 1) * 256, :], dqkv[...])
-
-    core_y, core_x = [], []
-    for ch in range(4):
-        part = qkv_term(1 - c, ch).astype(BF16)
-        for i in range(4):
-            put_yx(gs_y, gs_x, ch * 4 + i, part[i * 64 : i * 64 + 64])
-        where = pl.ds(ch * 2, 2)
-        core_y.append(links.send(gs_y.at[where], gr_y.at[where], mate))
-        where = (slice(None), pl.ds(ch * 64, 64), slice(None))
-        core_x.append(links.send(gs_x.at[where], gr_x.at[where], mate))
-    for ch in range(4):
-        part = qkv_term(c, ch).astype(BF16)
-        for i in range(4):
-            put_yx(s_y, s_x, ch * 4 + i, part[i * 64 : i * 64 + 64])
+    def y_term(h, dst):
+        for ch in range(4):
+            part = dot(hid_t[h, ch * 256 : (ch + 1) * 256, :], dqkv[:, :256]).astype(BF16)
+            for i in range(4):
+                at, side = (ch * 4 + i) // 2, (i % 2) * 64
+                dst[at, side : side + 64, :] = part[i * 64 : i * 64 + 64]
+
+    def x_term(h, dst):
+        for ch in range(4):
+            part = dot(hid_t[h, ch * 256 : (ch + 1) * 256, :], dqkv[:, 256:]).astype(BF16)
+            for i in range(4):
+                at = (ch * 4 + i) * 16
+                for qr in range(4):
+                    for ct in range(2):
+                        dst[qr * 2 + ct, at : at + 16, :] = part[
+                            i * 64 + qr * 16 : i * 64 + qr * 16 + 16, ct * 128 : ct * 128 + 128
+                        ]
+
+    def add(dst, more):
+        for k in range(8):
+            dst[k] = (dst[k].astype(F32) + more[k].astype(F32)).astype(BF16)
+
+    y_term(1 - c, gs_y)
+    core_y = links.send(gs_y, gr_y, mate)
+    x_term(1 - c, gs_x)
+    core_x = links.send(gs_x, gr_x, mate)
+    y_term(c, s_y)
     total = first_z.total()
     for k in range(8):
         s2_z[k] = total[k * 16 : k * 16 + 16]
     second_z = [links.send(s2_z.at[mod(y + d, 8)], r2_z.at[d - 1], at_y(d)) for d in range(1, 8)]
-    arrived(core_y)
-    for k in range(8):
-        s_y[k] = (s_y[k].astype(F32) + gr_y[k].astype(F32)).astype(BF16)
+    core_y.wait_recv()
+    add(s_y, gr_y)
     first_y = First(s_y, r_y, far_y, y, at_y)
-    arrived(core_x)
-    for k in range(8):
-        s_x[k] = (s_x[k].astype(F32) + gr_x[k].astype(F32)).astype(BF16)
+    x_term(c, s_x)
+    core_x.wait_recv()
+    add(s_x, gr_x)
     first_x = First(s_x, r_x, far_x, x, at_x)
 
     for n in range(4):
@@ -416,54 +449,63 @@
     r3_y[x] = summed(s2_y[z], r2_y, 7).astype(BF16)
     third_y = [links.send(r3_y.at[x], r3_y.at[x], at_x(d)) for d in range(1, 8)]
     arrived(second_x)
-    total = summed(s2_x[y], r2_x, 7).astype(BF16)
-    for k in range(2):
-        s3_x[k] = total[k * 16 : k * 16 + 16]
-    r3_x[z] = s3_x[zh]
-    third_x = [
-        links.send(s3_x.at[mod(z + d, 8) // 4], r3_x.at[z], at_z(d)) for d in range(1, 8)
-    ]
+    r3_x[z] = summed(s2_x[y], r2_x, 7).astype(BF16)
+    third_x = [links.send(r3_x.at[z], r3_x.at[z], at_z(d)) for d in range(1, 8)]
+
+    def squares(*pieces):
+        rows = [jnp.sum(piece * piece, axis=0, keepdims=True) for piece in pieces]
+        lanes = [row[:, i : i + 128] for row in rows for i in range(0, row.shape[1], 128)]
+        return sum(lanes[1:], lanes[0])
 
     arrived(third_y)
     fy[mine] = in_order(r3_y).astype(BF16)
-    spread += spread_zl(fy)
-    arrived(third_x)
-    tile = c * 8 + x
-    fx[tile] = in_order(r3_x).astype(BF16)
+    slot = c * 8 + z
+    nz[slot] = squares(fy[mine].astype(F32), fz[mine].astype(F32))
     spread += [
-        links.send(fx.at[tile], fx.at[tile], at_x(d, dc) if d else mate)
+        links.send(nz.at[slot], nz.at[slot], at_z(d, dc) if d else mate)
         for d in range(8)
         for dc in range(2)
         if d or dc
     ]
+    spread += spread_zl(fy)
+    arrived(third_x)
+    tile = c * 8 + x
+    both = in_order(r3_x).astype(BF16)
+    s3_x[0], s3_x[1] = both[:16], both[16:]
+    fx[tile] = s3_x[zh]
+    nx[tile] = squares(both.astype(F32))
+    for part in (nx, fx):
+        spread += [
+            links.send(part.at[tile], part.at[tile], at_x(d, dc) if d else mate)
+            for d in range(8)
+            for dc in range(2)
+            if d or dc
+        ]
     arrived(spread)
+    total = nz[0] + nx[0]
+    for i in range(1, 16):
+        total = total + (nz[i] + nx[i])
+    ny[y] = total
+    along = [links.send(ny.at[y], ny.at[y], at_y(d)) for d in range(1, 8)]
     for i in range(8):
         grads_ref[i * 16 : i * 16 + 16, 0:256] = fy[i].astype(F32)
         grads_ref[i * 16 : i * 16 + 16, 512:768] = fz[i].astype(F32)
         for ct in range(2):
             at = (i // 4) * 8 + (i % 4) * 2 + ct
             grads_ref[i * 16 : i * 16 + 16, 256 + ct * 128 : 384 + ct * 128] = fx[at].astype(F32)
-    whole = grads_ref[...]
-    square = (whole * whole).reshape(16, 8, 768).sum(axis=0)
-    tile_sum = square[:, 0:128]
-    for i in range(1, 6):
-        tile_sum = tile_sum + square[:, i * 128 : i * 128 + 128]
-    ny[own] = tile_sum
-    along = [links.send(ny.at[own], ny.at[own], at_y(d)) for d in range(1, 8)]
-    along += [links.send(ny.at[own], ny.at[own], across(d)) for d in range(8)]
     arrived(along)
     total = ny[0]
-    for i in range(1, 16):
+    for i in range(1, 8):
         total = total + ny[i]
     norm_ref[...] = total
     links.finish()
-    assert links.used <= SEMS
+    assert links.used <= SEMS, links.used
 
 
 def finish(ig_ref, grads_ref, tiles_ref, ig_out, update_ref, norm_ref, sem):
     store = pltpu.make_async_copy(ig_ref, ig_out, sem)
     store.start()
-    norm_sq = jnp.sum(jnp.sum(tiles_ref[...], axis=0, keepdims=True), axis=1, keepdims=True)
+    norm_sq = jnp.sum(tiles_ref[...], axis=1, keepdims=True)
     update_ref[...] = grads_ref[...] * lax.rsqrt(norm_sq / (D * 768) + 1e-06)
     norm_ref[...] = jnp.sqrt(norm_sq)
     store.wait()
@@ -486,7 +528,7 @@
 
     input_grad, grads, tiles = pl.pallas_call(
         kernel,
-        out_shape=(bf(ROWS, D), f32(128, 768), f32(8, 128)),
+        out_shape=(bf(ROWS, D), f32(128, 768), f32(1, 128)),
         in_specs=[smem, smem, vmem, vmem, hbm, hbm, hbm, hbm, hbm],
         out_specs=(vmem, vmem, vmem),
         scratch_shapes=[
@@ -521,7 +563,7 @@
             bf(7, 16, 256),
             bf(8, 16, 256),
             bf(2, 16, 128),
-            bf(8, 16, 128),
+            bf(8, 32, 128),
             bf(8, 16, 256),
             bf(128, 256),
             bf(256, 128),
@@ -529,9 +571,12 @@
             bf(8, 16, 256),
             bf(8, 16, 256),
             bf(16, 16, 128),
-            f32(16, 8, 128),
+            f32(16, 1, 128),
+            f32(16, 1, 128),
+            f32(8, 1, 128),
             pltpu.SemaphoreType.DMA((SEMS,)),
             pltpu.SemaphoreType.DMA((5,)),
+            pltpu.SemaphoreType.REGULAR((3, 4)),
         ],
         compiler_params=pltpu.CompilerParams(collective_id=0, has_side_effects=True),
         name="attention_backward",

time: 94.6 us -> 90.9 us (0.961)
  Pallas kernels: 93.1 us -> 89.5 us
    pallas_call x1, Pallas kernels: 91.4 us -> 87.7 us  [body(): pl.pallas_call(kernel, out_shape=(bf(ROWS, D), f32(128, 768), f32(1, 128)...]
where the time goes in v3:
time: 90.9 us; the launch traced here: 90.8 us
  Pallas kernels  89.5 us (98%)
  between operations  1.29 us (1%)
    pallas_call x1, Pallas kernels, body(): pl.pallas_call(kernel, out_shape=(bf(ROWS, D), f32(128, 768), f32(1, 128)...  87.7 us

profile of v3, /device:TPU:1, one launch (start us, length us, event | category | flops | bytes accessed | tf_op | source)
XLA Modules:
  0.0 90.8 jit_solution(83236707950970240)
XLA Ops:
  1.3 87.7 %attention_backward.1 = (bf16[256,2048]{1,0:T(8,128)(2,1)S(1)}, f32[128,768]{1,0:T(8,128)S(1)}, f32[1,128]{1,0:T(1,128)S(1)}) custom-call(s32[1]{0:T(128)S(6)} %copy.12.start_ref, s32[1,4]{1,0:T(1,128)} %doc_ref.1, f32[1,128]{1,0:T(1,128)} %constant.2.clone.inv_ref, f32[2,256]{1,0:T(2,128)} %bitcast.2, bf16[256,2048]{1,0:T(8,128)(2,1)} %hid_hbm.1, ...), custom_call_target="tpu_custom_call" | custom-call | tf_op jit(solution)/shard_map/attention_backward/pallas_call | solution.py:529
  89.0 1.7 %scaled_outputs.1 = (bf16[256,2048]{1,0:T(8,128)(2,1)}, f32[128,768]{1,0:T(8,128)}, f32[1,1]{1,0:T(1,128)}) custom-call(bf16[256,2048]{1,0:T(8,128)(2,1)S(1)} %get-tuple-element.9.ig_ref, f32[128,768]{1,0:T(8,128)S(1)} %get-tuple-element.10.grads_ref, f32[1,128]{1,0:T(1,128)S(1)} %get-tuple-element.11.tiles_ref), custom_call_target="tpu_custom_call" | custom-call | tf_op jit(solution)/shard_map/scaled_outputs/pallas_call | solution.py:594

commit v4 on v3

--- a/solution.py
+++ b/solution.py
@@ -15,7 +15,7 @@
 FSDP_REP = AXES
 F32 = jnp.float32
 BF16 = jnp.bfloat16
-SEMS = 540
+SEMS = 81
 
 
 def mod(value, size):
@@ -26,40 +26,50 @@
     return lax.dot_general(left, right, (contract, ((), ())), preferred_element_type=F32)
 
 
-class Links:
+MESH = pl.DeviceIdType.MESH
+
+
+class Flags:
     def __init__(self, sems):
-        self.sems, self.used, self.started = sems, 0, []
-
-    def send(self, src, dst, device):
-        at = self.used
-        self.used += 2
-        copy = pltpu.make_async_remote_copy(
-            src_ref=src,
-            dst_ref=dst,
-            send_sem=self.sems.at[at],
-            recv_sem=self.sems.at[at + 1],
-            device_id=device,
-            device_id_type=pl.DeviceIdType.MESH,
-        )
-        copy.start()
-        self.started.append(copy)
-        return copy
-
-    def finish(self):
-        for copy in self.started:
-            copy.wait_send()
-
-
-def arrived(copies):
-    for copy in copies:
-        copy.wait_recv()
+        self.sems, self.used = sems, 0
+
+    def take(self):
+        self.used += 1
+        return self.sems.at[self.used - 1]
+
+
+def start(src, dst, device, sent, got):
+    pltpu.make_async_remote_copy(
+        src_ref=src, dst_ref=dst, send_sem=sent, recv_sem=got, device_id=device, device_id_type=MESH
+    ).start()
+
+
+def await_bytes(whole, count, flag):
+    ref = whole.at[pl.ds(0, count)]
+    pltpu.make_async_copy(ref, ref, flag).wait()
+
+
+class Batch:
+    def __init__(self, flags, whole):
+        self.whole, self.sent, self.got, self.count = whole, flags.take(), flags.take(), 0
+
+    def send(self, src, dst, device, units=1):
+        start(src, dst, device, self.sent, self.got)
+        self.count += units
+        return self
+
+    def arrived(self):
+        await_bytes(self.whole, self.count, self.got)
+
+    def left(self):
+        await_bytes(self.whole, self.count, self.sent)
 
 
 def kernel(
-    start_ref,
-    doc_ref,
-    inv_ref,
-    lse_ref,
+    start_hbm,
+    doc_hbm,
+    inv_hbm,
+    lse_hbm,
     hid_hbm,
     og_hbm,
     as_hbm,
@@ -68,6 +78,10 @@
     ig_ref,
     grads_ref,
     norm_ref,
+    start_ref,
+    doc_ref,
+    inv_ref,
+    lse_ref,
     hid,
     og,
     saved,
@@ -146,7 +160,13 @@
     load_og = pltpu.make_async_copy(og_hbm, og, local.at[2])
     load_as = pltpu.make_async_copy(as_hbm, saved, local.at[3])
     load_hid = pltpu.make_async_copy(hid_hbm, hid, local.at[4])
-    for copy in (load_wq, load_wo, load_og, load_as, load_hid):
+    small = [
+        pltpu.make_async_copy(src, dst, local.at[5 + i])
+        for i, (src, dst) in enumerate(
+            ((start_hbm, start_ref), (inv_hbm, inv_ref), (lse_hbm, lse_ref), (doc_hbm, doc_ref))
+        )
+    ]
+    for copy in (load_wq, load_wo, *small, load_og, load_as, load_hid):
         copy.start()
     near = [mate, mirror]
     for at in (at_y, at_x, at_z):
@@ -154,7 +174,7 @@
     barrier = pltpu.get_barrier_semaphore()
 
     def tell(sem, device):
-        pl.semaphore_signal(sem, inc=1, device_id=device, device_id_type=pl.DeviceIdType.MESH)
+        pl.semaphore_signal(sem, inc=1, device_id=device, device_id_type=MESH)
 
     for peer in near:
         tell(barrier, peer)
@@ -173,42 +193,61 @@
 
     pass_word(0)
 
-    links = Links(sems)
-
-    def weight(block, first, count, device):
+    flags = Flags(sems)
+    weights_sent = flags.take()
+    rows_sent = []
+
+    def weight(block, first, count, device, got):
         ref = wbuf.at[rows_of(block, first, count), :]
-        return links.send(ref, ref, device)
+        start(ref, ref, device, weights_sent, got)
+        rows_sent.append(count)
 
     color = lax.rem(x, 2)
     base, other_base = color * 64 + c * 32, (1 - color) * 64 + c * 32
-    along_y = (at_y(1), at_y(-1))
+    along_y = {s: (at_y(s), at_y(-s)) for s in (1, 2)}
     along_x = (at_x(1), at_x(-1))
-    shared = []
+    across_x = (at_x(1, 1), at_x(-1, 1))
+    near_rows, far_rows = [], []
+    shared = [(flags.take(), near_rows)] * 3 + [(flags.take(), far_rows)] * 2
 
     class Ring:
-        def __init__(self, zside):
-            self.zside, self.beside = zside, {0: []}
-            self.sent = {(w, u): self.piece(0, u, along_y[w]) for u in range(2) for w in range(2)}
+        def __init__(self, zside, leap):
+            self.zside, self.leap = zside, leap
+            self.due = {s: {} for s in range(1, 5)}
+            self.beside = {s: (flags.take(), []) for s in range(5)}
+            for u in range(2):
+                for w in range(2):
+                    for s in (2, 1) if leap else (1,):
+                        self.piece(0, u, w, s, s)
 
         def block(self, d):
             return mod(y + d, 8) * 2 + self.zside
 
-        def piece(self, d, u, device):
-            return weight(self.block(d), base + 16 * u, 16, device)
+        def piece(self, d, u, w, s, hop):
+            self.due[s][w, u] = flags.take()
+            weight(self.block(d), base + 16 * u, 16, along_y[hop][w], self.due[s][w, u])
 
         def hand_over(self, d, u, s):
-            self.beside[s].append(self.piece(d, u, along_x[u]))
+            got, rows = self.beside[s]
+            for device in (along_x[u], across_x[u]) if s == 4 else (along_x[u],):
+                weight(self.block(d), base + 16 * u, 16, device, got)
+                rows.append(16)
 
         def to_mate(self, d, first):
-            shared.append(weight(self.block(d), first, 32, mate))
+            got, rows = shared[abs(d)]
+            weight(self.block(d), first, 32, mate, got)
+            rows.append(32)
 
         def step(self, s):
-            before, self.sent, self.beside[s] = self.sent, {}, []
-            for (w, u), copy in before.items():
-                copy.wait_recv()
+            for (w, u), got in self.due[s].items():
+                await_bytes(wbuf, 16, got)
                 d = s if w else -s
-                if s < 3 or (s == 3 and u == w):
-                    self.sent[w, u] = self.piece(d, u, along_y[w])
+                if self.leap and s == 2:
+                    if u == w:
+                        self.piece(d, u, w, 4, 2)
+                    self.piece(d, u, w, 3, 1)
+                elif not self.leap and (s < 3 or (s == 3 and u == w)):
+                    self.piece(d, u, w, s + 1, 1)
                 self.hand_over(d, u, s)
             self.mate_rows(s, base)
 
@@ -217,12 +256,17 @@
                 self.to_mate(d, first)
 
         def collect(self, s):
-            arrived(self.beside[s])
-            self.mate_rows(s, other_base)
-
-    ring_a = Ring(zh)
-    to_mirror = [weight(own, base + 16 * u, 16, mirror) for u in range(2)]
-
+            got, rows = self.beside[s]
+            await_bytes(wbuf, sum(rows), got)
+            if s < 4:
+                self.mate_rows(s, other_base)
+
+    ring_a = Ring(zh, False)
+    from_mirror = flags.take()
+    weight(own, base, 32, mirror, from_mirror)
+
+    for copy in small:
+        copy.wait()
     positions = (start_ref[0] + lax.broadcasted_iota(jnp.int32, (ROWS, HEAD), 0)).astype(F32)
     angles = positions * inv_ref[...]
     sign = jnp.where(lax.broadcasted_iota(jnp.int32, (ROWS, HEAD), 1) < HEAD // 2, -1.0, 1.0)
@@ -245,8 +289,8 @@
     load_as.wait()
     for j in range(8):
         transpose(og, og_t, j)
-    arrived(to_mirror)
-    ring_b = Ring(1 - zh)
+    await_bytes(wbuf, 32, from_mirror)
+    ring_b = Ring(1 - zh, True)
     for u in range(2):
         ring_b.hand_over(0, u, 0)
     ring_b.mate_rows(0, base)
@@ -259,23 +303,28 @@
     class First:
         def __init__(self, chunks, parts, relay, me, at):
             self.chunks, self.parts, self.relay, self.me, self.at = chunks, parts, relay, me, at
-            self.far = links.send(chunks.at[mod(me + 4, 8)], relay, at(sign_c))
-            self.sent = [self.go(i, d) for i, d in enumerate((-3, 2, -2, 1, -1))]
+            self.sent, self.got, self.far = flags.take(), flags.take(), flags.take()
+            start(chunks.at[mod(me + 4, 8)], relay, at(sign_c), self.sent, self.far)
+            for i, d in enumerate((-3, 2, -2, 1, -1)):
+                self.go(i, d)
 
         def go(self, i, d):
             there = mod(self.me + sign_c * d, 8)
-            return links.send(self.chunks.at[there], self.parts.at[i], self.at(sign_c * d))
+            start(self.chunks.at[there], self.parts.at[i], self.at(sign_c * d), self.sent, self.got)
 
         def pass_on(self):
-            self.far.wait_recv()
+            await_bytes(self.chunks, 1, self.far)
             there = mod(self.me + sign_c * 3, 8)
             both = self.chunks[there].astype(F32) + self.relay[...].astype(F32)
             self.chunks[there] = both.astype(BF16)
-            self.sent.append(self.go(5, 3))
+            self.go(5, 3)
 
         def total(self):
-            arrived(self.sent)
+            await_bytes(self.chunks, 6, self.got)
             return summed(self.chunks[self.me], self.parts, 6).astype(BF16)
+
+        def left(self):
+            await_bytes(self.chunks, 7, self.sent)
 
     def summed(own_part, parts, count):
         total = own_part.astype(F32)
@@ -302,41 +351,51 @@
         part = out_term(1 - c, ch).astype(BF16)
         for i in range(4):
             put_z(gs_z, ch * 4 + i, part[i * 64 : i * 64 + 64])
-    core_z = links.send(gs_z, gr_z, mate)
+    core_z = Batch(flags, gs_z).send(gs_z, gr_z, mate, 8)
     ring_a.collect(1)
+    ring_b.step(1)
+    ring_b.step(2)
     ring_a.step(3)
-    ring_b.step(1)
     hear(2)
     for ch in range(4):
         part = out_term(c, ch)
         for i in range(4):
             put_z(s_z, ch * 4 + i, part[i * 64 : i * 64 + 64].astype(BF16))
-    core_z.wait_recv()
+    core_z.arrived()
     for k in range(8):
         s_z[k] = (s_z[k].astype(F32) + gr_z[k].astype(F32)).astype(BF16)
     first_z = First(s_z, r_z, far_z, z, at_z)
     ring_a.collect(2)
     ring_b.collect(0)
+    ring_b.collect(1)
+    ring_b.step(3)
     ring_a.step(4)
-    ring_b.step(2)
     load_hid.wait()
     for j in range(4):
         transpose(hid, hid_t, j)
+    ring_b.step(4)
+    ring_b.collect(2)
     ring_a.collect(3)
-    ring_b.collect(1)
-    ring_b.step(3)
     first_z.pass_on()
     for j in range(4, 8):
         transpose(hid, hid_t, j)
+    ring_b.collect(3)
+    await_bytes(wbuf, sum(near_rows), shared[0][0])
+
+    def project(d, first=False):
+        rows = pl.ds(pl.multiple_of(mod(y + d, 8) * 256, 256), 256)
+        for src, cols in ((hid, slice(0, 512)), (og, slice(512, 768))):
+            part = dot(src[:, rows], wbuf[rows, cols])
+            proj[:, cols] = part if first else proj[:, cols] + part
+
+    project(0, True)
+    for d in (1, -1, 2, -2):
+        project(d)
     ring_a.collect(4)
-    ring_b.collect(2)
-    ring_b.step(4)
-    ring_b.collect(3)
     ring_b.collect(4)
-    arrived(shared)
-
-    proj[:, :512] = dot(hid[...], wbuf[:, :512])
-    proj[:, 512:] = dot(og[...], wbuf[:, 512:])
+    await_bytes(wbuf, sum(far_rows), shared[4][0])
+    for d in (3, -3, 4):
+        project(d)
     cosine, sines = cos_ref[...], sin_ref[...]
 
     def rotary(value):
@@ -397,19 +456,31 @@
             dst[k] = (dst[k].astype(F32) + more[k].astype(F32)).astype(BF16)
 
     y_term(1 - c, gs_y)
-    core_y = links.send(gs_y, gr_y, mate)
+    core_y = Batch(flags, gs_y).send(gs_y, gr_y, mate, 8)
     x_term(1 - c, gs_x)
-    core_x = links.send(gs_x, gr_x, mate)
+    core_x = Batch(flags, gs_x).send(gs_x, gr_x, mate, 8)
     y_term(c, s_y)
+    def exchange(parts, landing, me, at):
+        batch = Batch(flags, parts)
+        for d in range(1, 8):
+            batch.send(parts.at[mod(me + d, 8)], landing.at[d - 1], at(d))
+        return batch
+
+    def broadcast(pieces, me, devices):
+        batch = Batch(flags, pieces)
+        for device in devices:
+            batch.send(pieces.at[me], pieces.at[me], device)
+        return batch
+
     total = first_z.total()
     for k in range(8):
         s2_z[k] = total[k * 16 : k * 16 + 16]
-    second_z = [links.send(s2_z.at[mod(y + d, 8)], r2_z.at[d - 1], at_y(d)) for d in range(1, 8)]
-    core_y.wait_recv()
+    second_z = exchange(s2_z, r2_z, y, at_y)
+    core_y.arrived()
     add(s_y, gr_y)
     first_y = First(s_y, r_y, far_y, y, at_y)
     x_term(c, s_x)
-    core_x.wait_recv()
+    core_x.arrived()
     add(s_x, gr_x)
     first_x = First(s_x, r_x, far_x, x, at_x)
 
@@ -419,87 +490,81 @@
     first_y.pass_on()
     first_x.pass_on()
 
-    arrived(second_z)
+    await_bytes(wbuf, sum(rows_sent), weights_sent)
+    for batch in (core_z, core_y, core_x, first_z, second_z):
+        batch.left()
+    second_z.arrived()
     r3_z[x] = summed(s2_z[y], r2_z, 7).astype(BF16)
-    third_z = [links.send(r3_z.at[x], r3_z.at[x], at_x(d)) for d in range(1, 8)]
+    third_z = broadcast(r3_z, x, [at_x(d) for d in range(1, 8)])
 
     total = first_y.total()
     for k in range(8):
         s2_y[k] = total[k * 16 : k * 16 + 16]
-    second_y = [links.send(s2_y.at[mod(z + d, 8)], r2_y.at[d - 1], at_z(d)) for d in range(1, 8)]
+    second_y = exchange(s2_y, r2_y, z, at_z)
     total = first_x.total()
     for k in range(8):
         s2_x[k] = total[k * 32 : k * 32 + 32]
-    second_x = [links.send(s2_x.at[mod(y + d, 8)], r2_x.at[d - 1], at_y(d)) for d in range(1, 8)]
-
-    def spread_zl(pieces):
-        return [
-            links.send(pieces.at[mine], pieces.at[mine], at_zl(d, dc) if d else mate)
-            for d in range(4)
-            for dc in range(2)
-            if d or dc
-        ]
+    second_x = exchange(s2_x, r2_x, y, at_y)
+
+    beside_zl = [at_zl(d, dc) if d else mate for d in range(4) for dc in range(2) if d or dc]
+    beside_z = [at_z(d, dc) if d else mate for d in range(8) for dc in range(2) if d or dc]
+    beside_x = [at_x(d, dc) if d else mate for d in range(8) for dc in range(2) if d or dc]
 
     mine = c * 4 + zl
-    arrived(third_z)
+    third_z.arrived()
     fz[mine] = in_order(r3_z).astype(BF16)
-    spread = spread_zl(fz)
-
-    arrived(second_y)
+    spread = [broadcast(fz, mine, beside_zl)]
+
+    second_y.arrived()
     r3_y[x] = summed(s2_y[z], r2_y, 7).astype(BF16)
-    third_y = [links.send(r3_y.at[x], r3_y.at[x], at_x(d)) for d in range(1, 8)]
-    arrived(second_x)
+    third_y = broadcast(r3_y, x, [at_x(d) for d in range(1, 8)])
+    second_x.arrived()
     r3_x[z] = summed(s2_x[y], r2_x, 7).astype(BF16)
-    third_x = [links.send(r3_x.at[z], r3_x.at[z], at_z(d)) for d in range(1, 8)]
+    third_x = broadcast(r3_x, z, [at_z(d) for d in range(1, 8)])
 
     def squares(*pieces):
         rows = [jnp.sum(piece * piece, axis=0, keepdims=True) for piece in pieces]
         lanes = [row[:, i : i + 128] for row in rows for i in range(0, row.shape[1], 128)]
         return sum(lanes[1:], lanes[0])
 
-    arrived(third_y)
+    first_y.left()
+    first_x.left()
+    third_y.arrived()
     fy[mine] = in_order(r3_y).astype(BF16)
     slot = c * 8 + z
     nz[slot] = squares(fy[mine].astype(F32), fz[mine].astype(F32))
-    spread += [
-        links.send(nz.at[slot], nz.at[slot], at_z(d, dc) if d else mate)
-        for d in range(8)
-        for dc in range(2)
-        if d or dc
-    ]
-    spread += spread_zl(fy)
-    arrived(third_x)
+    spread.append(broadcast(nz, slot, beside_z))
+    spread.append(broadcast(fy, mine, beside_zl))
+    third_x.arrived()
     tile = c * 8 + x
     both = in_order(r3_x).astype(BF16)
     s3_x[0], s3_x[1] = both[:16], both[16:]
     fx[tile] = s3_x[zh]
     nx[tile] = squares(both.astype(F32))
-    for part in (nx, fx):
-        spread += [
-            links.send(part.at[tile], part.at[tile], at_x(d, dc) if d else mate)
-            for d in range(8)
-            for dc in range(2)
-            if d or dc
-        ]
-    arrived(spread)
+    spread.append(broadcast(nx, tile, beside_x))
+    spread.append(broadcast(fx, tile, beside_x))
+    for batch in spread:
+        batch.arrived()
     total = nz[0] + nx[0]
     for i in range(1, 16):
         total = total + (nz[i] + nx[i])
     ny[y] = total
-    along = [links.send(ny.at[y], ny.at[y], at_y(d)) for d in range(1, 8)]
+    along = broadcast(ny, y, [at_y(d) for d in range(1, 8)])
     for i in range(8):
         grads_ref[i * 16 : i * 16 + 16, 0:256] = fy[i].astype(F32)
         grads_ref[i * 16 : i * 16 + 16, 512:768] = fz[i].astype(F32)
         for ct in range(2):
             at = (i // 4) * 8 + (i % 4) * 2 + ct
             grads_ref[i * 16 : i * 16 + 16, 256 + ct * 128 : 384 + ct * 128] = fx[at].astype(F32)
-    arrived(along)
+    for batch in (second_y, second_x, third_z, third_y, third_x, *spread):
+        batch.left()
+    along.arrived()
     total = ny[0]
     for i in range(1, 8):
         total = total + ny[i]
     norm_ref[...] = total
-    links.finish()
-    assert links.used <= SEMS, links.used
+    along.left()
+    assert flags.used <= SEMS, flags.used
 
 
 def finish(ig_ref, grads_ref, tiles_ref, ig_out, update_ref, norm_ref, sem):
@@ -514,7 +579,6 @@
 def body(hidden_in, out_grad, attn_saved, row_lse, w_qkv, w_out_t, doc_lengths, seq_start):
     power = np.arange(HEAD // 2, dtype=np.float64) * 2.0 / HEAD
     inverse = np.tile(1000000.0 ** (-power), 2).astype(np.float32)[None, :]
-    smem = pl.BlockSpec(memory_space=pltpu.SMEM)
     vmem = pl.BlockSpec(memory_space=pltpu.VMEM)
     hbm = pl.BlockSpec(memory_space=pl.ANY)
     half = (8, 128, 256)
@@ -529,9 +593,13 @@
     input_grad, grads, tiles = pl.pallas_call(
         kernel,
         out_shape=(bf(ROWS, D), f32(128, 768), f32(1, 128)),
-        in_specs=[smem, smem, vmem, vmem, hbm, hbm, hbm, hbm, hbm],
+        in_specs=[hbm] * 9,
         out_specs=(vmem, vmem, vmem),
         scratch_shapes=[
+            pltpu.SMEM((1,), jnp.int32),
+            pltpu.SMEM((1, 4), jnp.int32),
+            f32(1, HEAD),
+            f32(2, ROWS),
             bf(ROWS, D),
             bf(ROWS, D),
             bf(ROWS, 256),
@@ -575,7 +643,7 @@
             f32(16, 1, 128),
             f32(8, 1, 128),
             pltpu.SemaphoreType.DMA((SEMS,)),
-            pltpu.SemaphoreType.DMA((5,)),
+            pltpu.SemaphoreType.DMA((9,)),
             pltpu.SemaphoreType.REGULAR((3, 4)),
         ],
         compiler_params=pltpu.CompilerParams(collective_id=0, has_side_effects=True),

time: 90.9 us -> 79.7 us (0.88)
  Pallas kernels: 89.5 us -> 78.3 us
    pallas_call x1, Pallas kernels: 87.7 us -> 76.6 us  [body(): pl.pallas_call(kernel, out_shape=(bf(ROWS, D), f32(128, 768), f32(1, 128)...]
where the time goes in v4:
time: 79.7 us; the launch traced here: 79.6 us
  Pallas kernels  78.3 us (98%)
  between operations  1.29 us (2%)
    pallas_call x1, Pallas kernels, body(): pl.pallas_call(kernel, out_shape=(bf(ROWS, D), f32(128, 768), f32(1, 128)...  76.6 us
    pallas_call x1, Pallas kernels, body(): pl.pallas_call(finish, out_shape=(jax.ShapeDtypeStruct((ROWS, D), BF16),...  1.73 us

profile of v4, /device:TPU:1, one launch (start us, length us, event | category | flops | bytes accessed | tf_op | source)
XLA Modules:
  0.0 79.6 jit_solution(7411370693291430172)
XLA Ops:
  1.3 76.6 %attention_backward.1 = (bf16[256,2048]{1,0:T(8,128)(2,1)S(1)}, f32[128,768]{1,0:T(8,128)S(1)}, f32[1,128]{1,0:T(1,128)S(1)}) custom-call(s32[1]{0:T(128)S(6)} %copy.12.start_hbm, s32[1,4]{1,0:T(1,128)} %doc_hbm.1, f32[1,128]{1,0:T(1,128)} %constant.2.clone.inv_hbm, f32[2,256]{1,0:T(2,128)} %bitcast.2, bf16[256,2048]{1,0:T(8,128)(2,1)} %hid_hbm.1, ...), custom_call_target="tpu_custom_call" | custom-call | tf_op jit(solution)/shard_map/attention_backward/pallas_call | solution.py:593
  77.8 1.7 %scaled_outputs.1 = (bf16[256,2048]{1,0:T(8,128)(2,1)}, f32[128,768]{1,0:T(8,128)}, f32[1,1]{1,0:T(1,128)}) custom-call(bf16[256,2048]{1,0:T(8,128)(2,1)S(1)} %get-tuple-element.9.ig_ref, f32[128,768]{1,0:T(8,128)S(1)} %get-tuple-element.10.grads_ref, f32[1,128]{1,0:T(1,128)S(1)} %get-tuple-element.11.tiles_ref), custom_call_target="tpu_custom_call" | custom-call | tf_op jit(solution)/shard_map/scaled_outputs/pallas_call | solution.py:662

commit v5 on v4

--- a/solution.py
+++ b/solution.py
@@ -15,7 +15,8 @@
 FSDP_REP = AXES
 F32 = jnp.float32
 BF16 = jnp.bfloat16
-SEMS = 81
+SEMS = 82
+FAR_FIRST = (4, 3, 5, 2, 6, 1, 7)
 
 
 def mod(value, size):
@@ -207,8 +208,9 @@
     along_y = {s: (at_y(s), at_y(-s)) for s in (1, 2)}
     along_x = (at_x(1), at_x(-1))
     across_x = (at_x(1, 1), at_x(-1, 1))
-    near_rows, far_rows = [], []
-    shared = [(flags.take(), near_rows)] * 3 + [(flags.take(), far_rows)] * 2
+    near_rows, third_rows, far_rows = [], [], []
+    shared = [(flags.take(), near_rows)] * 3
+    shared += [(flags.take(), third_rows), (flags.take(), far_rows)]
 
     class Ring:
         def __init__(self, zside, leap):
@@ -282,101 +284,101 @@
                 b = 2 * j + i
                 dst[h, b * 64 : (b + 1) * 64, :] = part[i * 128 + h * 64 : i * 128 + h * 64 + 64]
 
-    ring_a.step(1)
-    hear(0)
-    pass_word(1)
+    sign_c = 1 - 2 * c
+
+    class First:
+        def __init__(self, chunks, parts, relay, me, at):
+            self.chunks, self.parts, self.relay, self.me, self.at = chunks, parts, relay, me, at
+            self.sent, self.got, self.far = flags.take(), flags.take(), flags.take()
+            start(chunks.at[mod(me + 4, 8)], relay, at(sign_c), self.sent, self.far)
+            for i, d in enumerate((-3, 2, -2, -1)):
+                self.go(i, d)
+
+        def go(self, i, d):
+            there = mod(self.me + sign_c * d, 8)
+            start(self.chunks.at[there], self.parts.at[i], self.at(sign_c * d), self.sent, self.got)
+
+        def pass_on(self):
+            await_bytes(self.chunks, 1, self.far)
+            there = mod(self.me + sign_c * 3, 8)
+            both = self.chunks[there].astype(F32) + self.relay[...].astype(F32)
+            self.chunks[there] = both.astype(BF16)
+            self.go(4, 3)
+            self.go(5, 1)
+
+        def total(self):
+            await_bytes(self.chunks, 6, self.got)
+            return summed(self.chunks[self.me], self.parts, 6).astype(BF16)
+
+        def left(self):
+            await_bytes(self.chunks, 7, self.sent)
+
+    def summed(own_part, parts, count):
+        total = own_part.astype(F32)
+        for i in range(count):
+            total = total + parts[i].astype(F32)
+        return total
+
+    def in_order(parts):
+        total = parts[0].astype(F32)
+        for i in range(1, 8):
+            total = total + parts[i].astype(F32)
+        return total
+
+    def put_z(dst, block, tile):
+        for qr in range(4):
+            zz = (block % 2) * 4 + qr
+            yy = block // 2
+            dst[zz, yy * 16 : yy * 16 + 16, :] = tile[qr * 16 : qr * 16 + 16]
+
+    def out_term(h, ch):
+        return dot(og_t[h, ch * 256 : (ch + 1) * 256, :], saved[...])
+
     load_og.wait()
     load_as.wait()
     for j in range(8):
         transpose(og, og_t, j)
+    for ch in range(4):
+        part = out_term(1 - c, ch).astype(BF16)
+        for i in range(4):
+            put_z(gs_z, ch * 4 + i, part[i * 64 : i * 64 + 64])
+    core_z = Batch(flags, gs_z).send(gs_z, gr_z, mate, 8)
+    hear(0)
+    pass_word(1)
+    ring_a.step(1)
     await_bytes(wbuf, 32, from_mirror)
     ring_b = Ring(1 - zh, True)
     for u in range(2):
         ring_b.hand_over(0, u, 0)
     ring_b.mate_rows(0, base)
-    ring_a.step(2)
     hear(1)
     pass_word(2)
-
-    sign_c = 1 - 2 * c
-
-    class First:
-        def __init__(self, chunks, parts, relay, me, at):
-            self.chunks, self.parts, self.relay, self.me, self.at = chunks, parts, relay, me, at
-            self.sent, self.got, self.far = flags.take(), flags.take(), flags.take()
-            start(chunks.at[mod(me + 4, 8)], relay, at(sign_c), self.sent, self.far)
-            for i, d in enumerate((-3, 2, -2, 1, -1)):
-                self.go(i, d)
-
-        def go(self, i, d):
-            there = mod(self.me + sign_c * d, 8)
-            start(self.chunks.at[there], self.parts.at[i], self.at(sign_c * d), self.sent, self.got)
-
-        def pass_on(self):
-            await_bytes(self.chunks, 1, self.far)
-            there = mod(self.me + sign_c * 3, 8)
-            both = self.chunks[there].astype(F32) + self.relay[...].astype(F32)
-            self.chunks[there] = both.astype(BF16)
-            self.go(5, 3)
-
-        def total(self):
-            await_bytes(self.chunks, 6, self.got)
-            return summed(self.chunks[self.me], self.parts, 6).astype(BF16)
-
-        def left(self):
-            await_bytes(self.chunks, 7, self.sent)
-
-    def summed(own_part, parts, count):
-        total = own_part.astype(F32)
-        for i in range(count):
-            total = total + parts[i].astype(F32)
-        return total
-
-    def in_order(parts):
-        total = parts[0].astype(F32)
-        for i in range(1, 8):
-            total = total + parts[i].astype(F32)
-        return total
-
-    def put_z(dst, block, tile):
-        for qr in range(4):
-            zz = (block % 2) * 4 + qr
-            yy = block // 2
-            dst[zz, yy * 16 : yy * 16 + 16, :] = tile[qr * 16 : qr * 16 + 16]
-
-    def out_term(h, ch):
-        return dot(og_t[h, ch * 256 : (ch + 1) * 256, :], saved[...])
-
     for ch in range(4):
-        part = out_term(1 - c, ch).astype(BF16)
+        part = out_term(c, ch)
         for i in range(4):
-            put_z(gs_z, ch * 4 + i, part[i * 64 : i * 64 + 64])
-    core_z = Batch(flags, gs_z).send(gs_z, gr_z, mate, 8)
+            put_z(s_z, ch * 4 + i, part[i * 64 : i * 64 + 64].astype(BF16))
+    ring_a.step(2)
+    hear(2)
+    core_z.arrived()
+    for k in range(8):
+        s_z[k] = (s_z[k].astype(F32) + gr_z[k].astype(F32)).astype(BF16)
+    first_z = First(s_z, r_z, far_z, z, at_z)
     ring_a.collect(1)
     ring_b.step(1)
     ring_b.step(2)
     ring_a.step(3)
-    hear(2)
-    for ch in range(4):
-        part = out_term(c, ch)
-        for i in range(4):
-            put_z(s_z, ch * 4 + i, part[i * 64 : i * 64 + 64].astype(BF16))
-    core_z.arrived()
-    for k in range(8):
-        s_z[k] = (s_z[k].astype(F32) + gr_z[k].astype(F32)).astype(BF16)
-    first_z = First(s_z, r_z, far_z, z, at_z)
     ring_a.collect(2)
     ring_b.collect(0)
     ring_b.collect(1)
     ring_b.step(3)
     ring_a.step(4)
+    first_z.pass_on()
     load_hid.wait()
     for j in range(4):
         transpose(hid, hid_t, j)
     ring_b.step(4)
     ring_b.collect(2)
     ring_a.collect(3)
-    first_z.pass_on()
     for j in range(4, 8):
         transpose(hid, hid_t, j)
     ring_b.collect(3)
@@ -391,11 +393,13 @@
     project(0, True)
     for d in (1, -1, 2, -2):
         project(d)
+    await_bytes(wbuf, sum(third_rows), shared[3][0])
+    for d in (3, -3):
+        project(d)
     ring_a.collect(4)
     ring_b.collect(4)
     await_bytes(wbuf, sum(far_rows), shared[4][0])
-    for d in (3, -3, 4):
-        project(d)
+    project(4)
     cosine, sines = cos_ref[...], sin_ref[...]
 
     def rotary(value):
@@ -462,7 +466,7 @@
     y_term(c, s_y)
     def exchange(parts, landing, me, at):
         batch = Batch(flags, parts)
-        for d in range(1, 8):
+        for d in FAR_FIRST:
             batch.send(parts.at[mod(me + d, 8)], landing.at[d - 1], at(d))
         return batch
 
@@ -476,10 +480,10 @@
     for k in range(8):
         s2_z[k] = total[k * 16 : k * 16 + 16]
     second_z = exchange(s2_z, r2_z, y, at_y)
+    x_term(c, s_x)
     core_y.arrived()
     add(s_y, gr_y)
     first_y = First(s_y, r_y, far_y, y, at_y)
-    x_term(c, s_x)
     core_x.arrived()
     add(s_x, gr_x)
     first_x = First(s_x, r_x, far_x, x, at_x)
@@ -495,7 +499,7 @@
         batch.left()
     second_z.arrived()
     r3_z[x] = summed(s2_z[y], r2_z, 7).astype(BF16)
-    third_z = broadcast(r3_z, x, [at_x(d) for d in range(1, 8)])
+    third_z = broadcast(r3_z, x, [at_x(d) for d in FAR_FIRST])
 
     total = first_y.total()
     for k in range(8):
@@ -506,9 +510,9 @@
         s2_x[k] = total[k * 32 : k * 32 + 32]
     second_x = exchange(s2_x, r2_x, y, at_y)
 
-    beside_zl = [at_zl(d, dc) if d else mate for d in range(4) for dc in range(2) if d or dc]
-    beside_z = [at_z(d, dc) if d else mate for d in range(8) for dc in range(2) if d or dc]
-    beside_x = [at_x(d, dc) if d else mate for d in range(8) for dc in range(2) if d or dc]
+    beside_zl = [at_zl(d, dc) for d in (2, 3, 1) for dc in range(2)] + [mate]
+    beside_z = [at_z(d, dc) for d in FAR_FIRST for dc in range(2)] + [mate]
+    beside_x = [at_x(d, dc) for d in FAR_FIRST for dc in range(2)] + [mate]
 
     mine = c * 4 + zl
     third_z.arrived()
@@ -517,10 +521,10 @@
 
     second_y.arrived()
     r3_y[x] = summed(s2_y[z], r2_y, 7).astype(BF16)
-    third_y = broadcast(r3_y, x, [at_x(d) for d in range(1, 8)])
+    third_y = broadcast(r3_y, x, [at_x(d) for d in FAR_FIRST])
     second_x.arrived()
     r3_x[z] = summed(s2_x[y], r2_x, 7).astype(BF16)
-    third_x = broadcast(r3_x, z, [at_z(d) for d in range(1, 8)])
+    third_x = broadcast(r3_x, z, [at_z(d) for d in FAR_FIRST])
 
     def squares(*pieces):
         rows = [jnp.sum(piece * piece, axis=0, keepdims=True) for piece in pieces]
@@ -549,7 +553,7 @@
     for i in range(1, 16):
         total = total + (nz[i] + nx[i])
     ny[y] = total
-    along = broadcast(ny, y, [at_y(d) for d in range(1, 8)])
+    along = broadcast(ny, y, [at_y(d) for d in FAR_FIRST])
     for i in range(8):
         grads_ref[i * 16 : i * 16 + 16, 0:256] = fy[i].astype(F32)
         grads_ref[i * 16 : i * 16 + 16, 512:768] = fz[i].astype(F32)
@@ -567,13 +571,18 @@
     assert flags.used <= SEMS, flags.used
 
 
-def finish(ig_ref, grads_ref, tiles_ref, ig_out, update_ref, norm_ref, sem):
-    store = pltpu.make_async_copy(ig_ref, ig_out, sem)
-    store.start()
+def finish(ig_ref, grads_ref, tiles_ref, ig_out, update_out, norm_out, update_ref, norm_ref, sems):
+    stores = [pltpu.make_async_copy(ig_ref, ig_out, sems.at[0])]
+    stores[0].start()
     norm_sq = jnp.sum(tiles_ref[...], axis=1, keepdims=True)
+    norm_ref[...] = jnp.sqrt(norm_sq)
     update_ref[...] = grads_ref[...] * lax.rsqrt(norm_sq / (D * 768) + 1e-06)
-    norm_ref[...] = jnp.sqrt(norm_sq)
-    store.wait()
+    stores.append(pltpu.make_async_copy(update_ref, update_out, sems.at[1]))
+    stores.append(pltpu.make_async_copy(norm_ref, norm_out, sems.at[2]))
+    for store in stores[1:]:
+        store.start()
+    for store in stores:
+        store.wait()
 
 
 def body(hidden_in, out_grad, attn_saved, row_lse, w_qkv, w_out_t, doc_lengths, seq_start):
@@ -667,8 +676,8 @@
             jax.ShapeDtypeStruct((1, 1), F32),
         ),
         in_specs=[vmem] * 3,
-        out_specs=(hbm, vmem, vmem),
-        scratch_shapes=[pltpu.SemaphoreType.DMA],
+        out_specs=(hbm, hbm, hbm),
+        scratch_shapes=[f32(128, 768), f32(1, 1), pltpu.SemaphoreType.DMA((3,))],
         compiler_params=pltpu.CompilerParams(vmem_limit_bytes=8 * 2**20),
         name="scaled_outputs",
     )(input_grad, grads, tiles)

time: 79.7 us -> 77.7 us (0.975)
  Pallas kernels: 78.3 us -> 76.3 us
    pallas_call x1, Pallas kernels: 76.6 us -> 75.1 us  [body(): pl.pallas_call(kernel, out_shape=(bf(ROWS, D), f32(128, 768), f32(1, 128)...]
where the time goes in v5:
time: 77.7 us; the launch traced here: 77.6 us
  Pallas kernels  76.3 us (98%)
  between operations  1.29 us (2%)
    pallas_call x1, Pallas kernels, body(): pl.pallas_call(kernel, out_shape=(bf(ROWS, D), f32(128, 768), f32(1, 128)...  75.1 us

profile of v5, /device:TPU:1, one launch (start us, length us, event | category | flops | bytes accessed | tf_op | source)
XLA Modules:
  0.0 77.6 jit_solution(9129204455543258470)
XLA Ops:
  1.3 75.1 %attention_backward.1 = (bf16[256,2048]{1,0:T(8,128)(2,1)S(1)}, f32[128,768]{1,0:T(8,128)S(1)}, f32[1,128]{1,0:T(1,128)S(1)}) custom-call(s32[1]{0:T(128)S(6)} %copy.12.start_hbm, s32[1,4]{1,0:T(1,128)} %doc_hbm.1, f32[1,128]{1,0:T(1,128)} %constant.2.clone.inv_hbm, f32[2,256]{1,0:T(2,128)} %bitcast.2, bf16[256,2048]{1,0:T(8,128)(2,1)} %hid_hbm.1, ...), custom_call_target="tpu_custom_call" | custom-call | tf_op jit(solution)/shard_map/attention_backward/pallas_call | solution.py:602
  76.4 1.1 %scaled_outputs.1 = (bf16[256,2048]{1,0:T(8,128)(2,1)}, f32[128,768]{1,0:T(8,128)}, f32[1,1]{1,0:T(1,128)}) custom-call(bf16[256,2048]{1,0:T(8,128)(2,1)S(1)} %get-tuple-element.9.ig_ref, f32[128,768]{1,0:T(8,128)S(1)} %get-tuple-element.10.grads_ref, f32[1,128]{1,0:T(1,128)S(1)} %get-tuple-element.11.tiles_ref), custom_call_target="tpu_custom_call" | custom-call | tf_op jit(solution)/shard_map/scaled_outputs/pallas_call | solution.py:671

commit v6 on v5

--- a/solution.py
+++ b/solution.py
@@ -231,9 +231,12 @@
 
         def hand_over(self, d, u, s):
             got, rows = self.beside[s]
-            for device in (along_x[u], across_x[u]) if s == 4 else (along_x[u],):
+            for device in (along_x[u], across_x[u]) if self.direct(s) else (along_x[u],):
                 weight(self.block(d), base + 16 * u, 16, device, got)
                 rows.append(16)
+
+        def direct(self, s):
+            return self.leap and s == 4
 
         def to_mate(self, d, first):
             got, rows = shared[abs(d)]
@@ -260,7 +263,7 @@
         def collect(self, s):
             got, rows = self.beside[s]
             await_bytes(wbuf, sum(rows), got)
-            if s < 4:
+            if not self.direct(s):
                 self.mate_rows(s, other_base)
 
     ring_a = Ring(zh, False)
@@ -382,6 +385,7 @@
     for j in range(4, 8):
         transpose(hid, hid_t, j)
     ring_b.collect(3)
+    ring_a.collect(4)
     await_bytes(wbuf, sum(near_rows), shared[0][0])
 
     def project(d, first=False):
@@ -396,7 +400,6 @@
     await_bytes(wbuf, sum(third_rows), shared[3][0])
     for d in (3, -3):
         project(d)
-    ring_a.collect(4)
     ring_b.collect(4)
     await_bytes(wbuf, sum(far_rows), shared[4][0])
     project(4)
@@ -547,13 +550,16 @@
     nx[tile] = squares(both.astype(F32))
     spread.append(broadcast(nx, tile, beside_x))
     spread.append(broadcast(fx, tile, beside_x))
-    for batch in spread:
-        batch.arrived()
+    from_z, from_x = spread[1], spread[3]
+    from_z.arrived()
+    from_x.arrived()
     total = nz[0] + nx[0]
     for i in range(1, 16):
         total = total + (nz[i] + nx[i])
     ny[y] = total
     along = broadcast(ny, y, [at_y(d) for d in FAR_FIRST])
+    for batch in (spread[0], spread[2], spread[4]):
+        batch.arrived()
     for i in range(8):
         grads_ref[i * 16 : i * 16 + 16, 0:256] = fy[i].astype(F32)
         grads_ref[i * 16 : i * 16 + 16, 512:768] = fz[i].astype(F32)

time: 77.7 us -> 77.6 us (level)
  no operation moved by 1% of the time
where the time goes in v6:
time: 77.6 us; the launch traced here: 77.4 us
  Pallas kernels  76.1 us (98%)
  between operations  1.29 us (2%)
    pallas_call x1, Pallas kernels, body(): pl.pallas_call(kernel, out_shape=(bf(ROWS, D), f32(128, 768), f32(1, 128)...  75 us

profile of v6, /device:TPU:1, one launch (start us, length us, event | category | flops | bytes accessed | tf_op | source)
XLA Modules:
  0.0 77.4 jit_solution(4819505220338754840)
XLA Ops:
  1.3 75.0 %attention_backward.1 = (bf16[256,2048]{1,0:T(8,128)(2,1)S(1)}, f32[128,768]{1,0:T(8,128)S(1)}, f32[1,128]{1,0:T(1,128)S(1)}) custom-call(s32[1]{0:T(128)S(6)} %copy.12.start_hbm, s32[1,4]{1,0:T(1,128)} %doc_hbm.1, f32[1,128]{1,0:T(1,128)} %constant.2.clone.inv_hbm, f32[2,256]{1,0:T(2,128)} %bitcast.2, bf16[256,2048]{1,0:T(8,128)(2,1)} %hid_hbm.1, ...), custom_call_target="tpu_custom_call" | custom-call | tf_op jit(solution)/shard_map/attention_backward/pallas_call | solution.py:608
  76.3 1.1 %scaled_outputs.1 = (bf16[256,2048]{1,0:T(8,128)(2,1)}, f32[128,768]{1,0:T(8,128)}, f32[1,1]{1,0:T(1,128)}) custom-call(bf16[256,2048]{1,0:T(8,128)(2,1)S(1)} %get-tuple-element.9.ig_ref, f32[128,768]{1,0:T(8,128)S(1)} %get-tuple-element.10.grads_ref, f32[1,128]{1,0:T(1,128)S(1)} %get-tuple-element.11.tiles_ref), custom_call_target="tpu_custom_call" | custom-call | tf_op jit(solution)/shard_map/scaled_outputs/pallas_call | solution.py:677
